TPU v7x, 512 devices: a whole 4x8x8 slice. The times are simulated.
512 devices in a mesh: samp: 64 (over z, x, y_hi), feat: 8 (over y_lo, core).
Axes of the slice: x: 4, y: 8 (y_hi: 2, y_lo: 4; y = y_hi * 4 + y_lo), z: 8, core: 2. Of those that a mesh axis runs over, the one named last changes fastest.
Arguments:
- design_matrix: bfloat16 [8192, 32768], P('samp', 'feat'), may hold values from -0.09375 to 0.09375
- labels: int32 [8192], P('samp'), may hold values from 0 to 1
- weights: float32 [16, 32768], P(None, ('feat', 'samp')), may hold values from -6 to 6
- lambdas: float32 [16], replicated, may hold values from 0.05 to 1
- sketch: bfloat16 [32768, 384], P(('feat', 'samp')), may hold values from -0.03125 to 0.03125
- sketch_values: float32 [384], replicated, may hold values from 0.05 to 2
Outputs:
- new_weights: float32 [16, 32768], P(None, ('feat', 'samp'))
All inputs are finite; a program needn't handle non-finite values.
Results may differ from a plain program's by a relative error of at most 0.004.
Values may be sent and summed in bfloat16 or wider, within the bound.
A program may use at most 64 MiB of HBM per device.

v0:
```python
import functools

import jax
import jax.numpy as jnp
from jax import lax
from jax.sharding import Mesh
from jax.sharding import PartitionSpec as P

ITERS = 2
SAMP = ("samp_0", "samp_1", "samp_2")
FEAT = ("feat_0", "feat_1")
SAMP_FEAT = ("samp_0", "samp_1", "samp_2", "feat_0", "feat_1")
FEAT_SAMP = ("feat_0", "feat_1", "samp_0", "samp_1", "samp_2")


def laid_out(blocks, dim):
    blocks = jnp.moveaxis(blocks, 0, dim)
    shape = blocks.shape
    return blocks.reshape(*shape[:dim], shape[dim] * shape[dim + 1], *shape[dim + 2 :])


def from_everyone(value, axis):
    copies = jnp.broadcast_to(value, (lax.axis_size(axis), *value.shape))
    return lax.all_to_all(copies, axis, split_axis=0, concat_axis=0, tiled=True)


def gathered_copies(value, axis, dim):
    return laid_out(from_everyone(value, axis), dim)


def of_everyone(value, axis):
    everything = from_everyone(value, axis)
    return jnp.sum(everything, axis=0)


def in_blocks(value, dim, devices):
    before, after = (value.shape[:dim], value.shape[dim + 1 :])
    return jnp.moveaxis(value.reshape(*before, devices, -1, *after), dim, 0)


def summed_on_arrival(value, axis, dim):
    blocks = in_blocks(value, dim, lax.axis_size(axis))
    arrived = lax.all_to_all(blocks, axis, split_axis=0, concat_axis=0, tiled=True)
    return arrived.sum(axis=0)


def by_axis(value, axes):
    return functools.reduce(lax.psum, axes, value)


def shards(design_matrix, labels, weights, lambdas, sketch, sketch_values):
    sketch_full = sketch.astype(jnp.float32)
    smallest = jnp.min(sketch_values)
    ratios = (smallest + lambdas[:, None]) / (sketch_values[None, :] + lambdas[:, None]) - 1.0

    def apply_rows(vector):
        vector_half = vector.astype(jnp.bfloat16)
        partial_rows = lax.dot_general(
            gathered_copies(vector_half, SAMP, 1),
            design_matrix,
            (((1,), (1,)), ((), ())),
            preferred_element_type=jnp.float32,
        )
        return of_everyone(partial_rows, FEAT)

    def apply_columns(values):
        return summed_on_arrival(
            lax.dot_general(
                design_matrix, values, (((0,), (1,)), ((), ())), preferred_element_type=jnp.float32
            ),
            SAMP,
            0,
        ).T

    def precondition(residual):
        projected = jnp.dot(residual, sketch_full, precision=lax.Precision.HIGHEST)
        projected, squares = (
            by_axis(projected, SAMP_FEAT),
            by_axis(jnp.sum(residual * residual, axis=1), SAMP_FEAT),
        )
        correction = lax.dot_general(
            ratios * projected,
            sketch_full,
            (((1,), (1,)), ((), ())),
            precision=lax.Precision.HIGHEST,
        )
        precond_res = residual + correction
        res_dot = squares + jnp.sum(ratios * projected * projected, axis=1)
        return (precond_res, res_dot)

    logits = apply_rows(weights)
    probability = jax.nn.sigmoid(logits)
    hessian_diag = probability * (1.0 - probability)
    miss_rows = (probability - labels[None, :].astype(jnp.float32)).astype(jnp.bfloat16)
    gradient = apply_columns(miss_rows) + lambdas[:, None] * weights
    residual = -gradient
    precond_res, res_dot = precondition(residual)
    direction = precond_res
    update = jnp.zeros_like(residual)
    for iteration in range(ITERS):
        image_rows = apply_rows(direction)
        hess_dir = (
            apply_columns((hessian_diag * image_rows).astype(jnp.bfloat16))
            + lambdas[:, None] * direction
        )
        curvature = by_axis(jnp.sum(direction * hess_dir, axis=1), SAMP_FEAT)
        step_size = res_dot / curvature
        update = update + step_size[:, None] * direction
        if iteration + 1 < ITERS:
            residual = residual - step_size[:, None] * hess_dir
            precond_res, new_dot = precondition(residual)
            direction = precond_res + (new_dot / res_dot)[:, None] * direction
            res_dot = new_dot
    return weights + update


def solution(mesh):
    finer = Mesh(
        mesh.devices.reshape(8, 4, 2, 4, 2), ("samp_0", "samp_1", "samp_2", "feat_0", "feat_1")
    )
    placed = (P(SAMP, FEAT), P(SAMP), P(None, FEAT_SAMP), P(), P(FEAT_SAMP, None), P())
    return jax.shard_map(
        shards, mesh=finer, in_specs=placed, out_specs=P(None, FEAT_SAMP), check_vma=False
    )
```

profile of v0, /device:TPU:1, one launch (start us, length us, event | category | flops | bytes accessed | tf_op | source)
XLA Modules:
  0.0 434.0 jit_solution(9530558202284032506)
XLA Ops:
  0.0 0.8 convert_element_type.23
  1.0 33.0 %all_to_all.45 = bf16[64,2,512]{2,1,0:T(2,128)(2,1)S(1)} all-to-all(bf16[64,2,512]{2,1,0:T(2,128)(2,1)S(1)} %reshape.33), channel_id=1, replica_groups=mesh['samp_0'=8,'samp_1'=4,'samp_2'=2,'feat_0'=4,'feat_1'=2] {'samp_0','..., dimensions={0} | all-to-all | bytes 262144 | tf_op jit(solution)/shard_map/all_to_all | solution.py:24
  34.0 0.2 reshape.34
  34.3 0.3 reshape.27
  34.6 0.4 fusion.18
  35.0 0.6 broadcast_in_dim.13
  35.6 5.4 %all-to-all-start.1 = ((f32[8,16,128]{2,1,0:T(8,128)}), f32[8,16,128]{2,1,0:T(8,128)S(1)}, u32[]{:S(2)}, u32[]{:S(2)}) async-start(f32[8,16,128]{2,1,0:T(8,128)} %broadcast_in_dim.13), calls=%async_computation.1 | async-start | bytes 131072 | tf_op jit(solution)/shard_map/all_to_all | solution.py:24
  41.0 5.1 %all-to-all-done.1 = f32[8,16,128]{2,1,0:T(8,128)S(1)} async-done(((f32[8,16,128]{2,1,0:T(8,128)}), f32[8,16,128]{2,1,0:T(8,128)S(1)}, u32[]{:S(2)}, u32[]{:S(2)}) %all-to-all-start.1) | async-done | bytes 65568 | tf_op jit(solution)/shard_map/all_to_all | solution.py:24
  46.1 0.3 convolution_bitcast_fusion.2
  46.4 0.2 reshape.28
  46.6 0.3 copy.24
  46.9 1.0 reshape.35
  47.9 4.7 %all-to-all-start.2 = ((f32[64,1,1024]{2,1,0:T(1,128)}), f32[64,1,1024]{2,1,0:T(1,128)S(1)}, u32[]{:S(2)}, u32[]{:S(2)}) async-start(f32[64,1,1024]{2,1,0:T(1,128)} %reshape.35), calls=%async_computation.2 | async-start | bytes 524288 | tf_op jit(solution)/shard_map/all_to_all | solution.py:43
  52.7 0.6 reduce_min.9
  53.3 0.6 broadcast_add_fusion
  54.0 12.8 %all-to-all-done.2 = f32[64,1,1024]{2,1,0:T(1,128)S(1)} async-done(((f32[64,1,1024]{2,1,0:T(1,128)}), f32[64,1,1024]{2,1,0:T(1,128)S(1)}, u32[]{:S(2)}, u32[]{:S(2)}) %all-to-all-start.2) | async-done | bytes 262176 | tf_op jit(solution)/shard_map/all_to_all | solution.py:43
  66.8 0.5 broadcast.49
  67.3 1.3 reduce
  68.8 0.6 copy-done.2
  69.7 21.1 %psum.215 = f32[16,384]{1,0:T(8,128)S(1)} all-reduce(f32[16,384]{1,0:T(8,128)S(1)} %fusion.5), channel_id=1, replica_groups=mesh['samp_0'=8,'samp_1'=4,'samp_2'=2,'feat_0'=4,'feat_1'=2] {'samp_0'}, use_global_device_ids=true, to_apply=%region_9.0 | all-reduce | flops 6144 | bytes 49152 | tf_op jit(solution)/shard_map/psum | solution.py:48
  90.8 11.3 %psum.216 = f32[16,384]{1,0:T(8,128)S(1)} all-reduce(f32[16,384]{1,0:T(8,128)S(1)} %psum.215), channel_id=1, replica_groups=mesh['samp_0'=8,'samp_1'=4,'samp_2'=2,'feat_0'=4,'feat_1'=2] {'samp_1'}, use_global_device_ids=true, to_apply=%region_10.0 | all-reduce | flops 6144 | bytes 49152 | tf_op jit(solution)/shard_map/psum | solution.py:48
  102.1 12.7 %psum.217 = f32[16,384]{1,0:T(8,128)S(1)} all-reduce(f32[16,384]{1,0:T(8,128)S(1)} %psum.216), channel_id=1, replica_groups=mesh['samp_0'=8,'samp_1'=4,'samp_2'=2,'feat_0'=4,'feat_1'=2] {'samp_2'}, use_global_device_ids=true, to_apply=%region_11.0 | all-reduce | flops 6144 | bytes 49152 | tf_op jit(solution)/shard_map/psum | solution.py:48
  114.7 13.6 %psum.218 = f32[16,384]{1,0:T(8,128)S(1)} all-reduce(f32[16,384]{1,0:T(8,128)S(1)} %psum.217), channel_id=1, replica_groups=mesh['samp_0'=8,'samp_1'=4,'samp_2'=2,'feat_0'=4,'feat_1'=2] {'feat_0'}, use_global_device_ids=true, to_apply=%region_12.0 | all-reduce | flops 6144 | bytes 49152 | tf_op jit(solution)/shard_map/psum | solution.py:48
  128.3 20.3 %psum.219 = f32[16,384]{1,0:T(8,128)S(1)} all-reduce(f32[16,384]{1,0:T(8,128)S(1)} %psum.218), channel_id=1, replica_groups=mesh['samp_0'=8,'samp_1'=4,'samp_2'=2,'feat_0'=4,'feat_1'=2] {'feat_1'}, use_global_device_ids=true, to_apply=%region_13.0 | all-reduce | flops 6144 | bytes 49152 | tf_op jit(solution)/shard_map/psum | solution.py:48
  148.6 0.2 fusion.16
  149.1 24.1 %all_to_all.46 = bf16[64,2,512]{2,1,0:T(2,128)(2,1)S(1)} all-to-all(bf16[64,2,512]{2,1,0:T(2,128)(2,1)S(1)} %reshape.37), channel_id=1, replica_groups=mesh['samp_0'=8,'samp_1'=4,'samp_2'=2,'feat_0'=4,'feat_1'=2] {'samp_0','..., dimensions={0} | all-to-all | bytes 262144 | tf_op jit(solution)/shard_map/all_to_all | solution.py:24
  173.2 0.2 reshape.38
  173.5 0.3 reshape.29
  173.7 0.4 fusion.19
  174.1 9.0 %all_to_all.47 = f32[8,16,128]{2,1,0:T(8,128)S(1)} all-to-all(f32[8,16,128]{2,1,0:T(8,128)S(1)} %broadcast_in_dim.15), channel_id=1, replica_groups=mesh['samp_0'=8,'samp_1'=4,'samp_2'=2,'feat_0'=4,'feat_1'=2] {'feat_0','..., dimensions={0} | all-to-all | bytes 131072 | tf_op jit(solution)/shard_map/all_to_all | solution.py:24
  183.2 0.3 convolution_bitcast_fusion.1
  183.4 0.2 reshape.30
  183.6 0.3 copy.23
  184.0 1.0 reshape.39
  185.0 4.7 %all-to-all-start.5 = ((f32[64,1,1024]{2,1,0:T(1,128)}), f32[64,1,1024]{2,1,0:T(1,128)S(1)}, u32[]{:S(2)}, u32[]{:S(2)}) async-start(f32[64,1,1024]{2,1,0:T(1,128)} %reshape.39), calls=%async_computation.5 | async-start | bytes 524288 | tf_op jit(solution)/shard_map/all_to_all | solution.py:43
  189.8 13.9 %all-to-all-done.5 = f32[64,1,1024]{2,1,0:T(1,128)S(1)} async-done(((f32[64,1,1024]{2,1,0:T(1,128)}), f32[64,1,1024]{2,1,0:T(1,128)S(1)}, u32[]{:S(2)}, u32[]{:S(2)}) %all-to-all-start.5) | async-done | bytes 262176 | tf_op jit(solution)/shard_map/all_to_all | solution.py:43
  203.7 1.3 reduce.1
  205.4 11.7 %all-reduce.1 = (f32[16]{0:T(128)S(1)}, f32[16]{0:T(128)S(1)}) all-reduce(f32[16]{0:T(128)S(1)} %get-tuple-element.31, f32[16]{0:T(128)S(1)} %multiply_reduce_fusion.3), channel_id=1, replica_groups=mesh['samp_0'=8,'samp_1'=4,'samp_2'=2,'feat_0'=4,'feat_1'=2] {'samp_0'}, use_global_device_ids=true, to_apply=%region_3.0 | all-reduce | flops 32 | bytes 256 | tf_op jit(solution)/shard_map/psum | solution.py:48
  217.1 6.7 %all-reduce.5 = (f32[16]{0:T(128)S(1)}, f32[16]{0:T(128)S(1)}) all-reduce(f32[16]{0:T(128)S(1)} %get-tuple-element.7, f32[16]{0:T(128)S(1)} %get-tuple-element.8), channel_id=1, replica_groups=mesh['samp_0'=8,'samp_1'=4,'samp_2'=2,'feat_0'=4,'feat_1'=2] {'samp_1'}, use_global_device_ids=true, to_apply=%region_4.0 | all-reduce | flops 32 | bytes 256 | tf_op jit(solution)/shard_map/psum | solution.py:48
  223.8 7.8 %all-reduce.9 = (f32[16]{0:T(128)S(1)}, f32[16]{0:T(128)S(1)}) all-reduce(f32[16]{0:T(128)S(1)} %get-tuple-element.15, f32[16]{0:T(128)S(1)} %get-tuple-element.16), channel_id=1, replica_groups=mesh['samp_0'=8,'samp_1'=4,'samp_2'=2,'feat_0'=4,'feat_1'=2] {'samp_2'}, use_global_device_ids=true, to_apply=%region_5.0 | all-reduce | flops 32 | bytes 256 | tf_op jit(solution)/shard_map/psum | solution.py:48
  231.6 10.7 %all-reduce.3 = (f32[16]{0:T(128)S(1)}, f32[16]{0:T(128)S(1)}) all-reduce(f32[16]{0:T(128)S(1)} %get-tuple-element.23, f32[16]{0:T(128)S(1)} %get-tuple-element.24), channel_id=1, replica_groups=mesh['samp_0'=8,'samp_1'=4,'samp_2'=2,'feat_0'=4,'feat_1'=2] {'feat_0'}, use_global_device_ids=true, to_apply=%region_6.0 | all-reduce | flops 32 | bytes 256 | tf_op jit(solution)/shard_map/psum | solution.py:48
  242.3 12.2 %all-reduce.7 = (f32[16]{0:T(128)S(1)}, f32[16]{0:T(128)S(1)}) all-reduce(f32[16]{0:T(128)S(1)} %get-tuple-element.11, f32[16]{0:T(128)S(1)} %get-tuple-element.12), channel_id=1, replica_groups=mesh['samp_0'=8,'samp_1'=4,'samp_2'=2,'feat_0'=4,'feat_1'=2] {'feat_1'}, use_global_device_ids=true, to_apply=%region_7.0 | all-reduce | flops 32 | bytes 256 | tf_op jit(solution)/shard_map/psum | solution.py:48
  254.9 20.3 %all-reduce = (f32[16,384]{1,0:T(8,128)S(1)}, f32[16]{0:T(128)S(1)}) all-reduce(f32[16,384]{1,0:T(8,128)S(1)} %fusion.20, f32[16]{0:T(128)S(1)} %get-tuple-element.27), channel_id=1, replica_groups=mesh['samp_0'=8,'samp_1'=4,'samp_2'=2,'feat_0'=4,'feat_1'=2] {'samp_0'}, use_global_device_ids=true, to_apply=%region_29.0 | all-reduce | flops 6160 | bytes 49280 | tf_op jit(solution)/shard_map/psum | solution.py:48
  275.2 11.4 %all-reduce.4 = (f32[16,384]{1,0:T(8,128)S(1)}, f32[16]{0:T(128)S(1)}) all-reduce(f32[16,384]{1,0:T(8,128)S(1)} %get-tuple-element.5, f32[16]{0:T(128)S(1)} %get-tuple-element.6), channel_id=1, replica_groups=mesh['samp_0'=8,'samp_1'=4,'samp_2'=2,'feat_0'=4,'feat_1'=2] {'samp_1'}, use_global_device_ids=true, to_apply=%region_30.0 | all-reduce | flops 6160 | bytes 49280 | tf_op jit(solution)/shard_map/psum | solution.py:48
  286.6 9.8 %all-reduce.8 = (f32[16,384]{1,0:T(8,128)S(1)}, f32[16]{0:T(128)S(1)}) all-reduce(f32[16,384]{1,0:T(8,128)S(1)} %get-tuple-element.13, f32[16]{0:T(128)S(1)} %get-tuple-element.14), channel_id=1, replica_groups=mesh['samp_0'=8,'samp_1'=4,'samp_2'=2,'feat_0'=4,'feat_1'=2] {'samp_2'}, use_global_device_ids=true, to_apply=%region_31.0 | all-reduce | flops 6160 | bytes 49280 | tf_op jit(solution)/shard_map/psum | solution.py:48
  296.4 13.5 %all-reduce.2 = (f32[16,384]{1,0:T(8,128)S(1)}, f32[16]{0:T(128)S(1)}) all-reduce(f32[16,384]{1,0:T(8,128)S(1)} %get-tuple-element.21, f32[16]{0:T(128)S(1)} %get-tuple-element.22), channel_id=1, replica_groups=mesh['samp_0'=8,'samp_1'=4,'samp_2'=2,'feat_0'=4,'feat_1'=2] {'feat_0'}, use_global_device_ids=true, to_apply=%region_32.0 | all-reduce | flops 6160 | bytes 49280 | tf_op jit(solution)/shard_map/psum | solution.py:48
  309.9 19.8 %all-reduce.6 = (f32[16,384]{1,0:T(8,128)S(1)}, f32[16]{0:T(128)S(1)}) all-reduce(f32[16,384]{1,0:T(8,128)S(1)} %get-tuple-element.9, f32[16]{0:T(128)S(1)} %get-tuple-element.10), channel_id=1, replica_groups=mesh['samp_0'=8,'samp_1'=4,'samp_2'=2,'feat_0'=4,'feat_1'=2] {'feat_1'}, use_global_device_ids=true, to_apply=%region_33.0 | all-reduce | flops 6160 | bytes 49280 | tf_op jit(solution)/shard_map/psum | solution.py:48
  329.9 0.2 fusion.17
  330.4 22.1 %all_to_all.48 = bf16[64,2,512]{2,1,0:T(2,128)(2,1)S(1)} all-to-all(bf16[64,2,512]{2,1,0:T(2,128)(2,1)S(1)} %reshape.41), channel_id=1, replica_groups=mesh['samp_0'=8,'samp_1'=4,'samp_2'=2,'feat_0'=4,'feat_1'=2] {'samp_0','..., dimensions={0} | all-to-all | bytes 262144 | tf_op jit(solution)/shard_map/all_to_all | solution.py:24
  352.8 0.3 reshape.31
  353.0 0.4 fusion.21
  353.4 9.6 %all_to_all.49 = f32[8,16,128]{2,1,0:T(8,128)S(1)} all-to-all(f32[8,16,128]{2,1,0:T(8,128)S(1)} %broadcast_in_dim.34), channel_id=1, replica_groups=mesh['samp_0'=8,'samp_1'=4,'samp_2'=2,'feat_0'=4,'feat_1'=2] {'feat_0','..., dimensions={0} | all-to-all | bytes 131072 | tf_op jit(solution)/shard_map/all_to_all | solution.py:24
  363.0 0.3 convolution_bitcast_fusion
  363.3 0.2 reshape.32
  363.5 0.3 copy.22
  363.8 0.3 reshape.43
  364.1 18.5 %all_to_all.50 = f32[64,1,1024]{2,1,0:T(1,128)S(1)} all-to-all(f32[64,1,1024]{2,1,0:T(1,128)S(1)} %reshape.43), channel_id=1, replica_groups=mesh['samp_0'=8,'samp_1'=4,'samp_2'=2,'feat_0'=4,'feat_1'=2] {'samp_0','..., dimensions={0} | all-to-all | bytes 524288 | tf_op jit(solution)/shard_map/all_to_all | solution.py:43
  382.7 1.3 reduce.2
  384.4 11.7 %psum.235 = f32[16]{0:T(128)S(1)} all-reduce(f32[16]{0:T(128)S(1)} %fusion.4), channel_id=1, replica_groups=mesh['samp_0'=8,'samp_1'=4,'samp_2'=2,'feat_0'=4,'feat_1'=2] {'samp_0'}, use_global_device_ids=true, to_apply=%region_38.0 | all-reduce | flops 16 | bytes 128 | tf_op jit(solution)/shard_map/psum | solution.py:48
  396.0 6.7 %psum.236 = f32[16]{0:T(128)S(1)} all-reduce(f32[16]{0:T(128)S(1)} %psum.235), channel_id=1, replica_groups=mesh['samp_0'=8,'samp_1'=4,'samp_2'=2,'feat_0'=4,'feat_1'=2] {'samp_1'}, use_global_device_ids=true, to_apply=%region_39.0 | all-reduce | flops 16 | bytes 128 | tf_op jit(solution)/shard_map/psum | solution.py:48
  402.7 7.7 %psum.237 = f32[16]{0:T(128)S(1)} all-reduce(f32[16]{0:T(128)S(1)} %psum.236), channel_id=1, replica_groups=mesh['samp_0'=8,'samp_1'=4,'samp_2'=2,'feat_0'=4,'feat_1'=2] {'samp_2'}, use_global_device_ids=true, to_apply=%region_40.0 | all-reduce | flops 16 | bytes 128 | tf_op jit(solution)/shard_map/psum | solution.py:48
  410.4 10.7 %psum.238 = f32[16]{0:T(128)S(1)} all-reduce(f32[16]{0:T(128)S(1)} %psum.237), channel_id=1, replica_groups=mesh['samp_0'=8,'samp_1'=4,'samp_2'=2,'feat_0'=4,'feat_1'=2] {'feat_0'}, use_global_device_ids=true, to_apply=%region_41.0 | all-reduce | flops 16 | bytes 128 | tf_op jit(solution)/shard_map/psum | solution.py:48
  421.1 12.2 %psum.239 = f32[16]{0:T(128)S(1)} all-reduce(f32[16]{0:T(128)S(1)} %psum.238), channel_id=1, replica_groups=mesh['samp_0'=8,'samp_1'=4,'samp_2'=2,'feat_0'=4,'feat_1'=2] {'feat_1'}, use_global_device_ids=true, to_apply=%region_42.0 | all-reduce | flops 16 | bytes 128 | tf_op jit(solution)/shard_map/psum | solution.py:48
  433.3 0.7 add_add_fusion
  (44 shorter events, 3.3 us)
Async XLA Ops:
  0.0 34.6 %copy-start = (bf16[128,4096]{1,0:T(8,128)(2,1)S(1)}, bf16[128,4096]{1,0:T(8,128)(2,1)}, u32[]{:S(2)}) copy-start(bf16[128,4096]{1,0:T(8,128)(2,1)} %param.6) | copy-start | bytes 3145732
  35.6 5.4 %copy-start.5 = (s32[128]{0:T(128)S(1)}, s32[128]{0:T(128)}, u32[]{:S(2)}) copy-start(s32[128]{0:T(128)} %param.7) | copy-start | bytes 1540
  35.6 10.5 %all-to-all-start.1 = ((f32[8,16,128]{2,1,0:T(8,128)}), f32[8,16,128]{2,1,0:T(8,128)S(1)}, u32[]{:S(2)}, u32[]{:S(2)}) async-start(f32[8,16,128]{2,1,0:T(8,128)} %broadcast_in_dim.13), calls=%async_computation.1 | async-start | bytes 131072 | tf_op jit(solution)/shard_map/all_to_all | solution.py:24
  47.9 4.8 %copy-start.4 = (f32[384]{0:T(512)S(1)}, f32[384]{0:T(512)}, u32[]{:S(2)}) copy-start(f32[384]{0:T(512)} %param.11) | copy-start | bytes 4612
  47.9 18.9 %all-to-all-start.2 = ((f32[64,1,1024]{2,1,0:T(1,128)}), f32[64,1,1024]{2,1,0:T(1,128)S(1)}, u32[]{:S(2)}, u32[]{:S(2)}) async-start(f32[64,1,1024]{2,1,0:T(1,128)} %reshape.35), calls=%async_computation.2 | async-start | bytes 524288 | tf_op jit(solution)/shard_map/all_to_all | solution.py:43
  52.7 0.7 copy-start.3
  68.7 0.7 copy-start.2
  68.7 0.9 copy-start.1
  185.0 18.8 %all-to-all-start.5 = ((f32[64,1,1024]{2,1,0:T(1,128)}), f32[64,1,1024]{2,1,0:T(1,128)S(1)}, u32[]{:S(2)}, u32[]{:S(2)}) async-start(f32[64,1,1024]{2,1,0:T(1,128)} %reshape.39), calls=%async_computation.5 | async-start | bytes 524288 | tf_op jit(solution)/shard_map/all_to_all | solution.py:43
where the time goes:
time: 435 us; the launch traced here: 434 us
  blocking collectives  368 us (85%)
  waiting for transfers between devices  31.8 us (7%)
  starting transfers between devices  14.8 us (3%)
  local copies, waits for them, and re-layouts  8.54 us (2%)
  other arithmetic  7.91 us (2%)
    psum x20, blocking collectives, by_axis(): return functools.reduce(lax.psum, axes, value)  252 us
    all_to_all x5, blocking collectives, from_everyone(): return lax.all_to_all(copies, axis, split_axis=0, concat_axis=0, tiled=True)  97.7 us
    all_to_all x2, waiting for transfers between devices, summed_on_arrival(): lax.all_to_all(blocks, axis, split_axis=0, concat_axis=0, tiled=True)  26.7 us
    all_to_all x1, blocking collectives, summed_on_arrival(): lax.all_to_all(blocks, axis, split_axis=0, concat_axis=0, tiled=True)  18.5 us
    all_to_all x2, starting transfers between devices, summed_on_arrival(): lax.all_to_all(blocks, axis, split_axis=0, concat_axis=0, tiled=True)  9.4 us
  transfers between devices with their start and end apart: 3, of which 3 were waited for; matrix products, arithmetic and copies ran while one was open for 0% of the time, Pallas kernels for 0%

commit v1 on v0

v1 whole, which is shorter than its diff:
```python
import functools

import jax
import jax.numpy as jnp
from jax import lax
from jax.experimental import pallas as pl
from jax.experimental.pallas import tpu as pltpu
from jax.sharding import Mesh
from jax.sharding import PartitionSpec as P

SAMP = ("samp_0", "samp_1", "samp_2")
FEAT = ("feat_0", "feat_1")
FEAT_SAMP = FEAT + SAMP
F32, BF16 = jnp.float32, jnp.bfloat16
BY_LANES = (((1,), (1,)), ((), ()))
BY_ROWS = (((1,), (0,)), ((), ()))


def far_first(n):
    return sorted(range(n), key=lambda d: -min(d, n - d))


def split3(value):
    high = value.astype(BF16)
    rest = value - high.astype(F32)
    mid = rest.astype(BF16)
    low = (rest - mid.astype(F32)).astype(BF16)
    return jnp.concatenate([high, mid, low], axis=0)


def kernel(sizes, x_hbm, labels_ref, w_ref, lam_ref, s_hbm, sv_ref, out_ref,
           xv, sp, wb, ag, ags, ft, fts, fs, fss, rs, rss, yh, yhs, pr, prs, pz, pzs, pa, pas, kz, kzs, ky, kys,
           local_sem, send_sem, recv_sem):
    nz, nx, nh, nl, nc = sizes
    nzx, nf, ny = nz * nx, nl * nc, nh * nl * nc
    k, half = w_ref.shape
    wide = 2 * half
    rank = s_hbm.shape[1]
    z, x, h, l, c = (lax.axis_index(name) for name in SAMP + FEAT)
    zx, f, y = z * nx + x, l * nc + c, (h * nl + l) * nc + c

    copy_x = pltpu.make_async_copy(x_hbm, xv, local_sem.at[0])
    copy_x.start()
    copy_s = pltpu.make_async_copy(s_hbm, sp.at[h], local_sem.at[1])
    copy_s.start()

    zx_peers = []
    for dz in far_first(nz):
        for dx in far_first(nx):
            if dz or dx:
                zz, xx = lax.rem(z + dz, nz), lax.rem(x + dx, nx)
                zx_peers.append((zz * nx + xx, {"samp_0": zz, "samp_1": xx}))
    y_peers, f_peers = [], []
    for dl in far_first(nl):
        for dh in reversed(range(nh)):
            for dc in reversed(range(nc)):
                if dh or dl or dc:
                    hh, ll, cc = lax.rem(h + dh, nh), lax.rem(l + dl, nl), lax.rem(c + dc, nc)
                    y_peers.append(((hh * nl + ll) * nc + cc, {"samp_2": hh, "feat_0": ll, "feat_1": cc}))
                    if not dh:
                        f_peers.append((ll * nc + cc, {"feat_0": ll, "feat_1": cc}))
    partner = {"samp_2": 1 - h}

    barrier = pltpu.get_barrier_semaphore()
    for _, peer in zx_peers + y_peers:
        pl.semaphore_signal(barrier, inc=1, device_id=peer, device_id_type=pl.DeviceIdType.MESH)

    def copy(phase, src, dst, peer):
        return pltpu.make_async_remote_copy(
            src_ref=src, dst_ref=dst, send_sem=send_sem.at[phase], recv_sem=recv_sem.at[phase],
            device_id=peer, device_id_type=pl.DeviceIdType.MESH)

    sent = []

    def whole(phase, buffer, peer):
        arrived = copy(phase, buffer, buffer, peer)
        arrived.wait_recv()
        sent.append(arrived)

    lane = lax.broadcasted_iota(jnp.int32, (k, wide), 1)
    row = lax.broadcasted_iota(jnp.int32, (k, wide), 0)

    def pack(*columns):
        total = 0.0
        for place, column in enumerate(columns):
            total = total + jnp.where(lane == row + place * k, column, 0.0)
        return jnp.sum(total, axis=0, keepdims=True)

    def unpack(packed, place):
        return jnp.sum(jnp.where(lane == row + place * k, packed, 0.0), axis=1, keepdims=True)

    def lanes(value):
        return jnp.sum(value, axis=1, keepdims=True)

    def gather_start(i, value):
        ags[i] = value.astype(BF16)
        ag[i, zx] = value.astype(BF16)
        for _, peer in zx_peers:
            copy(2 + i, ags.at[i], ag.at[i, zx], peer).start()

    def gather_rows(i):
        whole(2 + i, ag.at[i, pl.ds(0, nzx - 1)], zx_peers[0][1])
        field = jnp.concatenate([ag[i, q] for q in range(nzx)], axis=1)
        return lax.dot_general(field, xv[...], BY_LANES, preferred_element_type=F32)

    def feat_sum(i, value):
        fts[i] = value
        ft[i, f] = value
        for _, peer in f_peers:
            copy(5 + i, fts.at[i], ft.at[i, f], peer).start()
        whole(5 + i, ft.at[i, pl.ds(0, nf - 1)], f_peers[0][1])
        return jnp.sum(ft[i], axis=0)

    def feat_scalars_start(i, value):
        fss[i] = value
        fs[i, f] = value
        for _, peer in f_peers:
            copy(8 + i, fss.at[i], fs.at[i, f], peer).start()

    def feat_scalars(i):
        whole(8 + i, fs.at[i, pl.ds(0, nf - 1)], f_peers[0][1])
        return jnp.sum(fs[i], axis=0)

    def column_sum(i, values):
        for dz in far_first(nz):
            zz = lax.rem(z + dz, nz)
            start = pl.multiple_of(zz * (nx * wide), nx * wide)
            part = lax.dot_general(values, xv[:, pl.ds(start, nx * wide)], BY_ROWS, preferred_element_type=F32)
            for xx in range(nx):
                rss[i, zz * nx + xx] = part[:, xx * wide:(xx + 1) * wide].astype(BF16)
            for dx in far_first(nx):
                if dz or dx:
                    xx = lax.rem(x + dx, nx)
                    copy(10 + i, rss.at[i, zz * nx + xx], rs.at[i, zx], {"samp_0": zz, "samp_1": xx}).start()
        rs[i, zx] = rss[i, zx]
        whole(10 + i, rs.at[i, pl.ds(0, nzx - 1)], zx_peers[0][1])
        return jnp.sum(rs[i].astype(F32), axis=0)

    def pair_start(i, value):
        yhs[i] = value
        copy(12 + i, yhs.at[i], yh.at[i], partner).start()

    def pair_sum(i, value):
        whole(12 + i, yh.at[i], partner)
        return value + yh[i]

    def project(i, value, scalars):
        parts = lax.dot_general(split3(value), sketch, BY_ROWS, preferred_element_type=F32)
        part = parts[:k] + parts[k:2 * k] + parts[2 * k:]
        for q in range(k):
            prs[i, q] = part[q:q + 1, :]
        for j, peer in y_peers:
            copy(14 + i, prs.at[i, j], pr.at[i, y], peer).start()
        pr[i, y] = prs[i, y]
        whole(14 + i, pr.at[i, pl.ds(0, ny - 1)], y_peers[0][1])
        mine = jnp.concatenate([jnp.sum(pr[i], axis=0), scalars], axis=1)
        pzs[i] = mine
        pz[i, zx] = mine
        for _, peer in zx_peers:
            copy(16 + i, pzs.at[i], pz.at[i, zx], peer).start()
        whole(16 + i, pz.at[i, pl.ds(0, nzx - 1)], zx_peers[0][1])
        mine = jnp.sum(pz[i], axis=0)
        pas[i] = mine
        pa[i, y] = mine
        for _, peer in y_peers:
            copy(18 + i, pas.at[i], pa.at[i, y], peer).start()
        whole(18 + i, pa.at[i, pl.ds(0, ny - 1)], y_peers[0][1])
        full = jnp.concatenate([pa[i, q] for q in range(k)], axis=0)
        return full[:, :rank], jnp.sum(full[:, rank:], axis=0, keepdims=True) * (1.0 / nf)

    def spread(projected):
        parts = lax.dot_general(split3(ratios * projected), sketch, BY_LANES, preferred_element_type=F32)
        return parts[:k] + parts[k:2 * k] + parts[2 * k:]

    lam = jnp.sum(jnp.where(lax.broadcasted_iota(jnp.int32, (k, k), 0) == lax.broadcasted_iota(jnp.int32, (k, k), 1),
                            lam_ref[...], 0.0), axis=1, keepdims=True)
    values = sv_ref[...]
    ratios = (jnp.min(values, axis=1, keepdims=True) + lam) / (values + lam) - 1.0
    wb[0, :, :half] = w_ref[...]
    wb[0, :, half:] = w_ref[...]
    pl.semaphore_wait(barrier, len(zx_peers) + len(y_peers))
    copy(0, wb.at[0], wb.at[1], partner).start()
    whole(0, wb.at[1], partner)
    own = (lane // half) == h
    weights = jnp.where(own, wb[0], wb[1])
    gather_start(0, weights)
    copy_s.wait()
    copy(1, sp.at[h], sp.at[h], partner).start()
    copy_x.wait()

    logits = feat_sum(0, gather_rows(0))
    probability = jax.nn.sigmoid(logits)
    diag = probability * (1.0 - probability)
    miss = (probability - labels_ref[...].astype(F32)).astype(BF16)
    part = -(column_sum(0, miss) + (0.5 * lam) * weights)
    pair_start(0, part)
    whole(1, sp.at[1 - h], partner)
    sketch = sp[...].reshape(2 * half, rank)
    projected, _ = project(0, part, jnp.zeros((1, wide), F32))
    residual = pair_sum(0, part)
    direction = residual + spread(projected)

    gather_start(1, direction)
    feat_scalars_start(0, pack(0.5 * lanes(residual * direction), 0.5 * lam * lanes(direction * direction)))
    image = feat_sum(1, gather_rows(1))
    scalars = feat_scalars(0) + pack(jnp.zeros((k, 1), F32), lanes(diag * image * image))
    part = column_sum(1, (diag * image).astype(BF16)) + (0.5 * lam) * direction
    pair_start(1, part)
    projected, scalars = project(1, part, scalars)
    hess_dir = pair_sum(1, part)
    hess_pre = hess_dir + spread(projected)
    res_dot, curvature = unpack(scalars, 0), unpack(scalars, 1)
    step = res_dot / curvature
    residual = residual - step * hess_dir
    precond = direction - step * hess_pre

    gather_start(2, precond)
    feat_scalars_start(1, pack(0.5 * lanes(residual * precond), 0.5 * lam * lanes(precond * precond),
                               0.5 * lam * lanes(precond * direction)))
    image_pre = feat_sum(2, gather_rows(2))
    mine = feat_scalars(1) + pack(jnp.zeros((k, 1), F32), lanes(diag * image_pre * image_pre),
                                  lanes(diag * image_pre * image))
    kzs[...] = mine
    kz[zx] = mine
    for _, peer in zx_peers:
        copy(20, kzs, kz.at[zx], peer).start()
    whole(20, kz.at[pl.ds(0, nzx - 1)], zx_peers[0][1])
    mine = jnp.sum(kz[...], axis=0)
    kys[...] = mine
    copy(21, kys, ky, partner).start()
    whole(21, ky, partner)
    scalars = mine + ky[...]
    new_dot, pre_pre, pre_dir = (unpack(scalars, place) for place in range(3))
    beta = new_dot / res_dot
    last = new_dot / (pre_pre + 2.0 * beta * pre_dir + beta * beta * curvature)
    out_ref[...] = step * direction + last * (precond + beta * direction)
    for arrived in sent:
        arrived.wait_send()


def shards(sizes, design_matrix, labels, weights, lambdas, sketch, sketch_values):
    nz, nx, nh, nl, nc = sizes
    nzx, nf, ny = nz * nx, nl * nc, nh * nl * nc
    k, half = weights.shape
    wide = 2 * half
    rank = sketch.shape[1]
    vmem = pl.BlockSpec(memory_space=pltpu.VMEM)
    anywhere = pl.BlockSpec(memory_space=pl.ANY)
    dma = pltpu.SemaphoreType.DMA
    update = pl.pallas_call(
        functools.partial(kernel, sizes),
        name="step",
        out_shape=jax.ShapeDtypeStruct((k, wide), F32),
        in_specs=[anywhere, vmem, vmem, vmem, anywhere, vmem],
        out_specs=vmem,
        scratch_shapes=[
            pltpu.VMEM(design_matrix.shape, BF16),
            pltpu.VMEM((2, half, rank), BF16),
            pltpu.VMEM((2, k, wide), F32),
            pltpu.VMEM((3, nzx, k, wide), BF16), pltpu.VMEM((3, k, wide), BF16),
            pltpu.VMEM((3, nf, k, wide), F32), pltpu.VMEM((3, k, wide), F32),
            pltpu.VMEM((2, nf, 1, wide), F32), pltpu.VMEM((2, 1, wide), F32),
            pltpu.VMEM((2, nzx, k, wide), BF16), pltpu.VMEM((2, nzx, k, wide), BF16),
            pltpu.VMEM((2, k, wide), F32), pltpu.VMEM((2, k, wide), F32),
            pltpu.VMEM((2, ny, 1, rank), F32), pltpu.VMEM((2, ny, 1, rank), F32),
            pltpu.VMEM((2, nzx, 1, rank + wide), F32), pltpu.VMEM((2, 1, rank + wide), F32),
            pltpu.VMEM((2, ny, 1, rank + wide), F32), pltpu.VMEM((2, 1, rank + wide), F32),
            pltpu.VMEM((nzx, 1, wide), F32), pltpu.VMEM((1, wide), F32),
            pltpu.VMEM((1, wide), F32), pltpu.VMEM((1, wide), F32),
            dma((2,)), dma((22,)), dma((22,)),
        ],
        compiler_params=pltpu.CompilerParams(collective_id=0, has_side_effects=True),
    )(design_matrix, labels.reshape(1, -1), weights, lambdas.reshape(1, -1), sketch, sketch_values.reshape(1, -1))
    return weights + lax.dynamic_slice_in_dim(update, lax.axis_index("samp_2") * half, half, axis=1)


def solution(mesh):
    sizes = (8, 4, 2, 4, 2)
    finer = Mesh(mesh.devices.reshape(sizes), SAMP + FEAT)
    placed = (P(SAMP, FEAT), P(SAMP), P(None, FEAT_SAMP), P(), P(FEAT_SAMP, None), P())
    return jax.shard_map(
        functools.partial(shards, sizes), mesh=finer, in_specs=placed, out_specs=P(None, FEAT_SAMP), check_vma=False
    )
```

time: 435 us -> 111 us (0.26)
  blocking collectives: 368 us -> 0 us
  Pallas kernels: 0 us -> 108 us
  waiting for transfers between devices: 31.8 us -> 0 us
  starting transfers between devices: 14.8 us -> 0 us
  local copies, waits for them, and re-layouts: 8.54 us -> 1.25 us
  other arithmetic: 7.91 us -> 1.38 us
    psum x20 -> x0, blocking collectives: 252 us -> none  [by_axis(): return functools.reduce(lax.psum, axes, value)]
    all_to_all x6 -> x0, blocking collectives: 116 us -> none  [the longest x5 97.7 us: from_everyone(): return lax.all_to_all(copies, axis, split_axis=0, concat_axis=0, tiled=True)]
    pallas_call x0 -> x1, Pallas kernels: none -> 108 us  [shards(): pl.pallas_call(functools.partial(kernel, sizes), name='step', out_shape=j...]
    all_to_all x3 -> x0, waiting for transfers between devices: 31.8 us -> none  [the longest x2 26.7 us: summed_on_arrival(): lax.all_to_all(blocks, axis, split_axis=0, concat_axis=0, tiled=True)]
    all_to_all x3 -> x0, starting transfers between devices: 14.8 us -> none  [the longest x2 9.4 us: summed_on_arrival(): lax.all_to_all(blocks, axis, split_axis=0, concat_axis=0, tiled=True)]
  transfers between devices with their start and end apart: 3 -> 0, of which waited for: 3 -> 0; matrix products, arithmetic and copies ran while one was open for 0% -> 0% of each run, Pallas kernels for 0% -> 0%
where the time goes in v1:
time: 111 us; the launch traced here: 110 us
  Pallas kernels  108 us (97%)
  other arithmetic  1.38 us (1%)
  local copies, waits for them, and re-layouts  1.25 us (1%)
    pallas_call x1, Pallas kernels, shards(): pl.pallas_call(functools.partial(kernel, sizes), name='step', out_shape=j...  108 us

profile of v1, /device:TPU:1, one launch (start us, length us, event | category | flops | bytes accessed | tf_op | source)
XLA Modules:
  0.0 110.4 jit_solution(17568448742023727847)
XLA Ops:
  0.0 0.0 copy-start.1
  0.0 0.7 copy-done.1
  0.7 0.6 reshape.11.sv_ref
  1.2 0.0 copy-start
  1.2 107.7 %step.1 = f32[16,128]{1,0:T(8,128)} custom-call(bf16[128,4096]{1,0:T(8,128)(2,1)} %x_hbm.1, s32[1,128]{1,0:T(1,128)} %bitcast.2, f32[16,64]{1,0:T(8,128)} %w_ref.1, f32[1,16]{1,0:T(1,128)} %bitcast.3, bf16[64,384]{1,0:T(8,128)(2,1)} %s_hbm.1, f32[1,384]{1,0:T(1,128)} %reshape.11.sv_ref), custom_call_target="tpu_custom_call" | custom-call | tf_op jit(solution)/shard_map/step/pallas_call | solution.py:250
  109.0 0.0 copy-done
  109.0 1.4 %dynamic-slice_add_fusion = f32[16,64]{1,0:T(8,128)} fusion(f32[16,64]{1,0:T(8,128)S(1)} %copy-done, f32[16,128]{1,0:T(8,128)} %step.1, s32[]{:T(128)S(6)} %select_n.3), kind=kLoop, calls=%fused_computation | loop fusion | flops 1024 | bytes 12292 | tf_op jit(solution)/shard_map/add | solution.py:274
Async XLA Ops:
  0.0 0.7 copy-start.1
  1.2 107.7 %copy-start = (f32[16,64]{1,0:T(8,128)S(1)}, f32[16,64]{1,0:T(8,128)}, u32[]{:S(2)}) copy-start(f32[16,64]{1,0:T(8,128)} %w_ref.1) | copy-start | bytes 12292

commit v2 on v1

--- a/solution.py
+++ b/solution.py
@@ -28,9 +28,9 @@
     return jnp.concatenate([high, mid, low], axis=0)
 
 
-def kernel(sizes, x_hbm, labels_ref, w_ref, lam_ref, s_hbm, sv_ref, out_ref,
-           xv, sp, wb, ag, ags, ft, fts, fs, fss, rs, rss, yh, yhs, pr, prs, pz, pzs, pa, pas, kz, kzs, ky, kys,
-           local_sem, send_sem, recv_sem):
+def kernel(sizes, x_hbm, labels_hbm, w_hbm, lam_hbm, s_hbm, sv_hbm, out_ref,
+           xv, labels_ref, w_ref, lam_ref, sv_ref, sp, wb, ag, ags, ft, fts, fs, fss, rs0, rss0, rs1, rss1, yh, yhs,
+           pr, prs, pz, pzs, pa, pas, kz, kzs, local_sem, send_sem, recv_sem, gather_sem):
     nz, nx, nh, nl, nc = sizes
     nzx, nf, ny = nz * nx, nl * nc, nh * nl * nc
     k, half = w_ref.shape
@@ -38,11 +38,6 @@
     rank = s_hbm.shape[1]
     z, x, h, l, c = (lax.axis_index(name) for name in SAMP + FEAT)
     zx, f, y = z * nx + x, l * nc + c, (h * nl + l) * nc + c
-
-    copy_x = pltpu.make_async_copy(x_hbm, xv, local_sem.at[0])
-    copy_x.start()
-    copy_s = pltpu.make_async_copy(s_hbm, sp.at[h], local_sem.at[1])
-    copy_s.start()
 
     zx_peers = []
     for dz in far_first(nz):
@@ -65,6 +60,11 @@
     for _, peer in zx_peers + y_peers:
         pl.semaphore_signal(barrier, inc=1, device_id=peer, device_id_type=pl.DeviceIdType.MESH)
 
+    loads = [pltpu.make_async_copy(src, dst, local_sem.at[j]) for j, (src, dst) in enumerate(
+        [(w_hbm, w_ref), (lam_hbm, lam_ref), (sv_hbm, sv_ref), (labels_hbm, labels_ref), (s_hbm, sp.at[h]), (x_hbm, xv)])]
+    for load in loads:
+        load.start()
+
     def copy(phase, src, dst, peer):
         return pltpu.make_async_remote_copy(
             src_ref=src, dst_ref=dst, send_sem=send_sem.at[phase], recv_sem=recv_sem.at[phase],
@@ -95,13 +95,27 @@
     def gather_start(i, value):
         ags[i] = value.astype(BF16)
         ag[i, zx] = value.astype(BF16)
-        for _, peer in zx_peers:
-            copy(2 + i, ags.at[i], ag.at[i, zx], peer).start()
+        for dz in far_first(nz):
+            for dx in far_first(nx):
+                if dz or dx:
+                    zz, xx = lax.rem(z + dz, nz), lax.rem(x + dx, nx)
+                    pltpu.make_async_remote_copy(
+                        src_ref=ags.at[i], dst_ref=ag.at[i, zx], send_sem=send_sem.at[2 + i], recv_sem=gather_sem.at[i, dz],
+                        device_id={"samp_0": zz, "samp_1": xx}, device_id_type=pl.DeviceIdType.MESH).start()
 
     def gather_rows(i):
-        whole(2 + i, ag.at[i, pl.ds(0, nzx - 1)], zx_peers[0][1])
-        field = jnp.concatenate([ag[i, q] for q in range(nzx)], axis=1)
-        return lax.dot_general(field, xv[...], BY_LANES, preferred_element_type=F32)
+        total = jnp.zeros((k, xv.shape[0]), F32)
+        for dz in reversed(far_first(nz)):
+            group = ag.at[i, pl.ds(0, nx if dz else nx - 1)]
+            pltpu.make_async_remote_copy(
+                src_ref=group, dst_ref=group, send_sem=send_sem.at[2 + i], recv_sem=gather_sem.at[i, dz],
+                device_id=zx_peers[0][1], device_id_type=pl.DeviceIdType.MESH).wait_recv()
+            zz = lax.rem(z + (nz - dz), nz)
+            field = jnp.concatenate([ag[i, zz * nx + q] for q in range(nx)], axis=1)
+            start = pl.multiple_of(zz * (nx * wide), nx * wide)
+            total = total + lax.dot_general(field, xv[:, pl.ds(start, nx * wide)], BY_LANES, preferred_element_type=F32)
+        sent.append(copy(2 + i, ag.at[i, pl.ds(0, nzx - 1)], ag.at[i, pl.ds(0, nzx - 1)], zx_peers[0][1]))
+        return total
 
     def feat_sum(i, value):
         fts[i] = value
@@ -122,19 +136,20 @@
         return jnp.sum(fs[i], axis=0)
 
     def column_sum(i, values):
+        rs, rss = ((rs0, rss0), (rs1, rss1))[i]
         for dz in far_first(nz):
             zz = lax.rem(z + dz, nz)
             start = pl.multiple_of(zz * (nx * wide), nx * wide)
             part = lax.dot_general(values, xv[:, pl.ds(start, nx * wide)], BY_ROWS, preferred_element_type=F32)
             for xx in range(nx):
-                rss[i, zz * nx + xx] = part[:, xx * wide:(xx + 1) * wide].astype(BF16)
+                rss[zz * nx + xx] = part[:, xx * wide:(xx + 1) * wide].astype(rss.dtype)
             for dx in far_first(nx):
                 if dz or dx:
                     xx = lax.rem(x + dx, nx)
-                    copy(10 + i, rss.at[i, zz * nx + xx], rs.at[i, zx], {"samp_0": zz, "samp_1": xx}).start()
-        rs[i, zx] = rss[i, zx]
-        whole(10 + i, rs.at[i, pl.ds(0, nzx - 1)], zx_peers[0][1])
-        return jnp.sum(rs[i].astype(F32), axis=0)
+                    copy(10 + i, rss.at[zz * nx + xx], rs.at[zx], {"samp_0": zz, "samp_1": xx}).start()
+        rs[zx] = rss[zx]
+        whole(10 + i, rs.at[pl.ds(0, nzx - 1)], zx_peers[0][1])
+        return jnp.sum(rs[...].astype(F32), axis=0)
 
     def pair_start(i, value):
         yhs[i] = value
@@ -172,9 +187,11 @@
         parts = lax.dot_general(split3(ratios * projected), sketch, BY_LANES, preferred_element_type=F32)
         return parts[:k] + parts[k:2 * k] + parts[2 * k:]
 
+    for load in loads[:4]:
+        load.wait()
     lam = jnp.sum(jnp.where(lax.broadcasted_iota(jnp.int32, (k, k), 0) == lax.broadcasted_iota(jnp.int32, (k, k), 1),
                             lam_ref[...], 0.0), axis=1, keepdims=True)
-    values = sv_ref[...]
+    values = sv_ref[...].reshape(1, rank)
     ratios = (jnp.min(values, axis=1, keepdims=True) + lam) / (values + lam) - 1.0
     wb[0, :, :half] = w_ref[...]
     wb[0, :, half:] = w_ref[...]
@@ -184,9 +201,9 @@
     own = (lane // half) == h
     weights = jnp.where(own, wb[0], wb[1])
     gather_start(0, weights)
-    copy_s.wait()
+    loads[4].wait()
     copy(1, sp.at[h], sp.at[h], partner).start()
-    copy_x.wait()
+    loads[5].wait()
 
     logits = feat_sum(0, gather_rows(0))
     probability = jax.nn.sigmoid(logits)
@@ -221,15 +238,15 @@
     mine = feat_scalars(1) + pack(jnp.zeros((k, 1), F32), lanes(diag * image_pre * image_pre),
                                   lanes(diag * image_pre * image))
     kzs[...] = mine
-    kz[zx] = mine
-    for _, peer in zx_peers:
-        copy(20, kzs, kz.at[zx], peer).start()
-    whole(20, kz.at[pl.ds(0, nzx - 1)], zx_peers[0][1])
-    mine = jnp.sum(kz[...], axis=0)
-    kys[...] = mine
-    copy(21, kys, ky, partner).start()
-    whole(21, ky, partner)
-    scalars = mine + ky[...]
+    kz[zx * nh + h] = mine
+    for dh in reversed(range(nh)):
+        for dz in far_first(nz):
+            for dx in far_first(nx):
+                if dh or dz or dx:
+                    peer = {"samp_0": lax.rem(z + dz, nz), "samp_1": lax.rem(x + dx, nx), "samp_2": lax.rem(h + dh, nh)}
+                    copy(20, kzs, kz.at[zx * nh + h], peer).start()
+    whole(20, kz.at[pl.ds(0, nzx * nh - 1)], partner)
+    scalars = jnp.sum(kz[...], axis=0)
     new_dot, pre_pre, pre_dir = (unpack(scalars, place) for place in range(3))
     beta = new_dot / res_dot
     last = new_dot / (pre_pre + 2.0 * beta * pre_dir + beta * beta * curvature)
@@ -251,26 +268,28 @@
         functools.partial(kernel, sizes),
         name="step",
         out_shape=jax.ShapeDtypeStruct((k, wide), F32),
-        in_specs=[anywhere, vmem, vmem, vmem, anywhere, vmem],
+        in_specs=[anywhere] * 6,
         out_specs=vmem,
         scratch_shapes=[
             pltpu.VMEM(design_matrix.shape, BF16),
+            pltpu.VMEM((1, design_matrix.shape[0]), jnp.int32), pltpu.VMEM((k, half), F32), pltpu.VMEM((1, k), F32),
+            pltpu.VMEM((rank,), F32),
             pltpu.VMEM((2, half, rank), BF16),
             pltpu.VMEM((2, k, wide), F32),
             pltpu.VMEM((3, nzx, k, wide), BF16), pltpu.VMEM((3, k, wide), BF16),
             pltpu.VMEM((3, nf, k, wide), F32), pltpu.VMEM((3, k, wide), F32),
             pltpu.VMEM((2, nf, 1, wide), F32), pltpu.VMEM((2, 1, wide), F32),
-            pltpu.VMEM((2, nzx, k, wide), BF16), pltpu.VMEM((2, nzx, k, wide), BF16),
+            pltpu.VMEM((nzx, k, wide), F32), pltpu.VMEM((nzx, k, wide), F32),
+            pltpu.VMEM((nzx, k, wide), BF16), pltpu.VMEM((nzx, k, wide), BF16),
             pltpu.VMEM((2, k, wide), F32), pltpu.VMEM((2, k, wide), F32),
             pltpu.VMEM((2, ny, 1, rank), F32), pltpu.VMEM((2, ny, 1, rank), F32),
             pltpu.VMEM((2, nzx, 1, rank + wide), F32), pltpu.VMEM((2, 1, rank + wide), F32),
             pltpu.VMEM((2, ny, 1, rank + wide), F32), pltpu.VMEM((2, 1, rank + wide), F32),
-            pltpu.VMEM((nzx, 1, wide), F32), pltpu.VMEM((1, wide), F32),
-            pltpu.VMEM((1, wide), F32), pltpu.VMEM((1, wide), F32),
-            dma((2,)), dma((22,)), dma((22,)),
+            pltpu.VMEM((nzx * nh, 1, wide), F32), pltpu.VMEM((1, wide), F32),
+            dma((6,)), dma((21,)), dma((21,)), dma((3, nz)),
         ],
         compiler_params=pltpu.CompilerParams(collective_id=0, has_side_effects=True),
-    )(design_matrix, labels.reshape(1, -1), weights, lambdas.reshape(1, -1), sketch, sketch_values.reshape(1, -1))
+    )(design_matrix, labels.reshape(1, -1), weights, lambdas.reshape(1, -1), sketch, sketch_values)
     return weights + lax.dynamic_slice_in_dim(update, lax.axis_index("samp_2") * half, half, axis=1)
 
 

time: 111 us -> 110 us (level)
  local copies, waits for them, and re-layouts: 1.25 us -> 0.01 us
where the time goes in v2:
time: 110 us; the launch traced here: 109 us
  Pallas kernels  108 us (98%)
  other arithmetic  1.38 us (1%)
    pallas_call x1, Pallas kernels, shards(): pl.pallas_call(functools.partial(kernel, sizes), name='step', out_shape=j...  108 us

profile of v2, /device:TPU:1, one launch (start us, length us, event | category | flops | bytes accessed | tf_op | source)
XLA Modules:
  0.0 109.3 jit_solution(10028139743938088914)
XLA Ops:
  0.0 0.0 copy-start
  0.0 107.9 %step.1 = f32[16,128]{1,0:T(8,128)} custom-call(bf16[128,4096]{1,0:T(8,128)(2,1)} %x_hbm.1, s32[1,128]{1,0:T(1,128)} %bitcast.2, f32[16,64]{1,0:T(8,128)} %w_hbm.1, f32[1,16]{1,0:T(1,128)} %bitcast.3, bf16[64,384]{1,0:T(8,128)(2,1)} %s_hbm.1, f32[384]{0:T(512)} %sv_hbm.1), custom_call_target="tpu_custom_call" | custom-call | tf_op jit(solution)/shard_map/step/pallas_call | solution.py:267
  107.9 0.0 copy-done
  107.9 1.4 %dynamic-slice_add_fusion = f32[16,64]{1,0:T(8,128)} fusion(f32[16,64]{1,0:T(8,128)S(1)} %copy-done, f32[16,128]{1,0:T(8,128)} %step.1, s32[]{:T(128)S(6)} %select_n.3), kind=kLoop, calls=%fused_computation | loop fusion | flops 1024 | bytes 12292 | tf_op jit(solution)/shard_map/add | solution.py:293
Async XLA Ops:
  0.0 107.9 %copy-start = (f32[16,64]{1,0:T(8,128)S(1)}, f32[16,64]{1,0:T(8,128)}, u32[]{:S(2)}) copy-start(f32[16,64]{1,0:T(8,128)} %w_hbm.1) | copy-start | bytes 12292

commit v3 on v2

--- a/solution.py
+++ b/solution.py
@@ -29,8 +29,8 @@
 
 
 def kernel(sizes, x_hbm, labels_hbm, w_hbm, lam_hbm, s_hbm, sv_hbm, out_ref,
-           xv, labels_ref, w_ref, lam_ref, sv_ref, sp, wb, ag, ags, ft, fts, fs, fss, rs0, rss0, rs1, rss1, yh, yhs,
-           pr, prs, pz, pzs, pa, pas, kz, kzs, local_sem, send_sem, recv_sem, gather_sem):
+           xv, labels_ref, w_ref, lam_ref, sv_ref, sp, wb, ag, ags, ft, fts, fs, fss, rs0, rss0, rs1, rss1, xr, xs, yh, yhs,
+           pr, prs, pz, pzs, pa, pas, cz, czs, cf, kz, kzs, local_sem, send_sem, recv_sem, gather_sem):
     nz, nx, nh, nl, nc = sizes
     nzx, nf, ny = nz * nx, nl * nc, nh * nl * nc
     k, half = w_ref.shape
@@ -61,7 +61,7 @@
         pl.semaphore_signal(barrier, inc=1, device_id=peer, device_id_type=pl.DeviceIdType.MESH)
 
     loads = [pltpu.make_async_copy(src, dst, local_sem.at[j]) for j, (src, dst) in enumerate(
-        [(w_hbm, w_ref), (lam_hbm, lam_ref), (sv_hbm, sv_ref), (labels_hbm, labels_ref), (s_hbm, sp.at[h]), (x_hbm, xv)])]
+        [(w_hbm, w_ref), (lam_hbm, lam_ref), (sv_hbm, sv_ref), (labels_hbm, labels_ref), (s_hbm, sp.at[x * nh + h]), (x_hbm, xv)])]
     for load in loads:
         load.start()
 
@@ -103,18 +103,42 @@
                         src_ref=ags.at[i], dst_ref=ag.at[i, zx], send_sem=send_sem.at[2 + i], recv_sem=gather_sem.at[i, dz],
                         device_id={"samp_0": zz, "samp_1": xx}, device_id_type=pl.DeviceIdType.MESH).start()
 
+    def spread_start(i, value):
+        czs[i] = value.astype(BF16)
+        for dz in far_first(nz):
+            zz = lax.rem(z + dz, nz)
+            if dz:
+                pltpu.make_async_remote_copy(
+                    src_ref=czs.at[i], dst_ref=cz.at[i, z], send_sem=send_sem.at[23 + i], recv_sem=gather_sem.at[3 + i, dz],
+                    device_id={"samp_0": zz}, device_id_type=pl.DeviceIdType.MESH).start()
+
+    def arrived_group(phase, place, dz, group):
+        pltpu.make_async_remote_copy(
+            src_ref=group, dst_ref=group, send_sem=send_sem.at[phase], recv_sem=gather_sem.at[place, dz],
+            device_id=zx_peers[0][1], device_id_type=pl.DeviceIdType.MESH).wait_recv()
+
+    def rows_of(field, zz):
+        start = pl.multiple_of(zz * (nx * wide), nx * wide)
+        return lax.dot_general(field, xv[:, pl.ds(start, nx * wide)], BY_LANES, preferred_element_type=F32)
+
     def gather_rows(i):
         total = jnp.zeros((k, xv.shape[0]), F32)
         for dz in reversed(far_first(nz)):
-            group = ag.at[i, pl.ds(0, nx if dz else nx - 1)]
-            pltpu.make_async_remote_copy(
-                src_ref=group, dst_ref=group, send_sem=send_sem.at[2 + i], recv_sem=gather_sem.at[i, dz],
-                device_id=zx_peers[0][1], device_id_type=pl.DeviceIdType.MESH).wait_recv()
+            arrived_group(2 + i, i, dz, ag.at[i, pl.ds(0, nx if dz else nx - 1)])
             zz = lax.rem(z + (nz - dz), nz)
-            field = jnp.concatenate([ag[i, zz * nx + q] for q in range(nx)], axis=1)
-            start = pl.multiple_of(zz * (nx * wide), nx * wide)
-            total = total + lax.dot_general(field, xv[:, pl.ds(start, nx * wide)], BY_LANES, preferred_element_type=F32)
+            total = total + rows_of(jnp.concatenate([ag[i, zz * nx + q] for q in range(nx)], axis=1), zz)
         sent.append(copy(2 + i, ag.at[i, pl.ds(0, nzx - 1)], ag.at[i, pl.ds(0, nzx - 1)], zx_peers[0][1]))
+        return total
+
+    def spread_rows(i, total):
+        for dz in reversed(far_first(nz)):
+            zz = lax.rem(z + (nz - dz), nz)
+            if dz:
+                arrived_group(23 + i, 3 + i, dz, cz.at[i, 0])
+                total = total + rows_of(cz[i, zz], zz)
+            else:
+                total = total + rows_of(czs[i], zz)
+        sent.append(copy(23 + i, cz.at[i, pl.ds(0, nz - 1)], cz.at[i, pl.ds(0, nz - 1)], zx_peers[0][1]))
         return total
 
     def feat_sum(i, value):
@@ -135,57 +159,73 @@
         whole(8 + i, fs.at[i, pl.ds(0, nf - 1)], f_peers[0][1])
         return jnp.sum(fs[i], axis=0)
 
-    def column_sum(i, values):
+    def reduce_columns(i, values, state, scalars):
         rs, rss = ((rs0, rss0), (rs1, rss1))[i]
         for dz in far_first(nz):
             zz = lax.rem(z + dz, nz)
             start = pl.multiple_of(zz * (nx * wide), nx * wide)
             part = lax.dot_general(values, xv[:, pl.ds(start, nx * wide)], BY_ROWS, preferred_element_type=F32)
-            for xx in range(nx):
-                rss[zz * nx + xx] = part[:, xx * wide:(xx + 1) * wide].astype(rss.dtype)
-            for dx in far_first(nx):
-                if dz or dx:
-                    xx = lax.rem(x + dx, nx)
-                    copy(10 + i, rss.at[zz * nx + xx], rs.at[zx], {"samp_0": zz, "samp_1": xx}).start()
-        rs[zx] = rss[zx]
-        whole(10 + i, rs.at[pl.ds(0, nzx - 1)], zx_peers[0][1])
-        return jnp.sum(rs[...].astype(F32), axis=0)
-
-    def pair_start(i, value):
-        yhs[i] = value
-        copy(12 + i, yhs.at[i], yh.at[i], partner).start()
-
-    def pair_sum(i, value):
-        whole(12 + i, yh.at[i], partner)
-        return value + yh[i]
-
-    def project(i, value, scalars):
-        parts = lax.dot_general(split3(value), sketch, BY_ROWS, preferred_element_type=F32)
-        part = parts[:k] + parts[k:2 * k] + parts[2 * k:]
+            rss[zz] = part.astype(rss.dtype)
+            if dz:
+                copy(10 + i, rss.at[zz], rs.at[z], {"samp_0": zz}).start()
+        rs[z] = rss[z]
+        whole(10 + i, rs.at[pl.ds(0, nz - 1)], zx_peers[0][1])
+        along_z = jnp.sum(rs[...].astype(F32), axis=0)
+        ridge = (0.5 * lam) * state
+        chunks = [along_z[:, q * wide:(q + 1) * wide] + ridge * jnp.where(x == q, 1.0, 0.0) for q in range(nx)]
+
+        parts = lax.dot_general(split3(jnp.concatenate(chunks, axis=1)), sketch, BY_ROWS, preferred_element_type=F32)
+        projected = parts[:k] + parts[k:2 * k] + parts[2 * k:]
         for q in range(k):
-            prs[i, q] = part[q:q + 1, :]
+            prs[i, q] = projected[q:q + 1, :]
         for j, peer in y_peers:
             copy(14 + i, prs.at[i, j], pr.at[i, y], peer).start()
         pr[i, y] = prs[i, y]
+
+        for q in range(nx):
+            xs[i, q] = chunks[q]
+        for dx in far_first(nx):
+            xx = lax.rem(x + dx, nx)
+            if dx:
+                copy(21 + i, xs.at[i, xx], xr.at[i, x], {"samp_1": xx}).start()
+        xr[i, x] = xs[i, x]
+        whole(21 + i, xr.at[i, pl.ds(0, nx - 1)], {"samp_1": lax.rem(x + 1, nx)})
+        part = jnp.sum(xr[i], axis=0)
+        yhs[i] = part
+        copy(12 + i, yhs.at[i], yh.at[i], partner).start()
+
         whole(14 + i, pr.at[i, pl.ds(0, ny - 1)], y_peers[0][1])
-        mine = jnp.concatenate([jnp.sum(pr[i], axis=0), scalars], axis=1)
-        pzs[i] = mine
-        pz[i, zx] = mine
+        mine = jnp.sum(pr[i], axis=0)
+        if scalars is not None:
+            mine = jnp.concatenate([mine, scalars], axis=1)
+        across = slice(0, mine.shape[1])
+        pzs[i, :, across] = mine
+        pz[i, zx, :, across] = mine
         for _, peer in zx_peers:
-            copy(16 + i, pzs.at[i], pz.at[i, zx], peer).start()
-        whole(16 + i, pz.at[i, pl.ds(0, nzx - 1)], zx_peers[0][1])
-        mine = jnp.sum(pz[i], axis=0)
-        pas[i] = mine
-        pa[i, y] = mine
+            copy(16 + i, pzs.at[i, :, across], pz.at[i, zx, :, across], peer).start()
+
+        whole(12 + i, yh.at[i], partner)
+        vector = part + yh[i]
+        gather_start(1 + i, vector)
+
+        whole(16 + i, pz.at[i, pl.ds(0, nzx - 1), :, across], zx_peers[0][1])
+        mine = jnp.sum(pz[i, :, :, across], axis=0)
+        pas[i, :, across] = mine
+        pa[i, y, :, across] = mine
         for _, peer in y_peers:
-            copy(18 + i, pas.at[i], pa.at[i, y], peer).start()
-        whole(18 + i, pa.at[i, pl.ds(0, ny - 1)], y_peers[0][1])
-        full = jnp.concatenate([pa[i, q] for q in range(k)], axis=0)
-        return full[:, :rank], jnp.sum(full[:, rank:], axis=0, keepdims=True) * (1.0 / nf)
-
-    def spread(projected):
-        parts = lax.dot_general(split3(ratios * projected), sketch, BY_LANES, preferred_element_type=F32)
-        return parts[:k] + parts[k:2 * k] + parts[2 * k:]
+            copy(18 + i, pas.at[i, :, across], pa.at[i, y, :, across], peer).start()
+        image = gather_rows(1 + i)
+        whole(18 + i, pa.at[i, pl.ds(0, ny - 1), :, across], y_peers[0][1])
+        full = jnp.concatenate([pa[i, q, :, across] for q in range(k)], axis=0)
+        if scalars is not None:
+            scalars = jnp.sum(full[:, rank:], axis=0, keepdims=True) * (1.0 / nf)
+
+        parts = lax.dot_general(split3(ratios * full[:, :rank]), sketch, BY_LANES, preferred_element_type=F32)
+        correction = parts[:k] + parts[k:2 * k] + parts[2 * k:]
+        spread_start(i, correction)
+        for q in range(nx):
+            cf[i, q] = correction[:, q * wide:(q + 1) * wide]
+        return vector, vector + cf[i, x], image, scalars
 
     for load in loads[:4]:
         load.wait()
@@ -202,39 +242,32 @@
     weights = jnp.where(own, wb[0], wb[1])
     gather_start(0, weights)
     loads[4].wait()
-    copy(1, sp.at[h], sp.at[h], partner).start()
+    for dh in reversed(range(nh)):
+        for dx in far_first(nx):
+            if dh or dx:
+                peer = {"samp_1": lax.rem(x + dx, nx), "samp_2": lax.rem(h + dh, nh)}
+                copy(1, sp.at[x * nh + h], sp.at[x * nh + h], peer).start()
     loads[5].wait()
 
     logits = feat_sum(0, gather_rows(0))
     probability = jax.nn.sigmoid(logits)
     diag = probability * (1.0 - probability)
     miss = (probability - labels_ref[...].astype(F32)).astype(BF16)
-    part = -(column_sum(0, miss) + (0.5 * lam) * weights)
-    pair_start(0, part)
-    whole(1, sp.at[1 - h], partner)
-    sketch = sp[...].reshape(2 * half, rank)
-    projected, _ = project(0, part, jnp.zeros((1, wide), F32))
-    residual = pair_sum(0, part)
-    direction = residual + spread(projected)
-
-    gather_start(1, direction)
+    whole(1, sp.at[pl.ds(0, nx * nh - 1)], partner)
+    sketch = sp[...].reshape(nx * nh * half, rank)
+    gradient, gradient_pre, image, _ = reduce_columns(0, miss, weights, None)
+    residual, direction = -gradient, -gradient_pre
     feat_scalars_start(0, pack(0.5 * lanes(residual * direction), 0.5 * lam * lanes(direction * direction)))
-    image = feat_sum(1, gather_rows(1))
+    image = -feat_sum(1, spread_rows(0, image))
     scalars = feat_scalars(0) + pack(jnp.zeros((k, 1), F32), lanes(diag * image * image))
-    part = column_sum(1, (diag * image).astype(BF16)) + (0.5 * lam) * direction
-    pair_start(1, part)
-    projected, scalars = project(1, part, scalars)
-    hess_dir = pair_sum(1, part)
-    hess_pre = hess_dir + spread(projected)
+    hess_dir, hess_pre, image_pre, scalars = reduce_columns(1, (diag * image).astype(BF16), direction, scalars)
     res_dot, curvature = unpack(scalars, 0), unpack(scalars, 1)
     step = res_dot / curvature
     residual = residual - step * hess_dir
     precond = direction - step * hess_pre
-
-    gather_start(2, precond)
     feat_scalars_start(1, pack(0.5 * lanes(residual * precond), 0.5 * lam * lanes(precond * precond),
                                0.5 * lam * lanes(precond * direction)))
-    image_pre = feat_sum(2, gather_rows(2))
+    image_pre = image - step * feat_sum(2, spread_rows(1, image_pre))
     mine = feat_scalars(1) + pack(jnp.zeros((k, 1), F32), lanes(diag * image_pre * image_pre),
                                   lanes(diag * image_pre * image))
     kzs[...] = mine
@@ -274,19 +307,22 @@
             pltpu.VMEM(design_matrix.shape, BF16),
             pltpu.VMEM((1, design_matrix.shape[0]), jnp.int32), pltpu.VMEM((k, half), F32), pltpu.VMEM((1, k), F32),
             pltpu.VMEM((rank,), F32),
-            pltpu.VMEM((2, half, rank), BF16),
+            pltpu.VMEM((nx * nh, half, rank), BF16),
             pltpu.VMEM((2, k, wide), F32),
             pltpu.VMEM((3, nzx, k, wide), BF16), pltpu.VMEM((3, k, wide), BF16),
             pltpu.VMEM((3, nf, k, wide), F32), pltpu.VMEM((3, k, wide), F32),
             pltpu.VMEM((2, nf, 1, wide), F32), pltpu.VMEM((2, 1, wide), F32),
-            pltpu.VMEM((nzx, k, wide), F32), pltpu.VMEM((nzx, k, wide), F32),
-            pltpu.VMEM((nzx, k, wide), BF16), pltpu.VMEM((nzx, k, wide), BF16),
+            pltpu.VMEM((nz, k, nx * wide), F32), pltpu.VMEM((nz, k, nx * wide), F32),
+            pltpu.VMEM((nz, k, nx * wide), BF16), pltpu.VMEM((nz, k, nx * wide), BF16),
+            pltpu.VMEM((2, nx, k, wide), F32), pltpu.VMEM((2, nx, k, wide), F32),
             pltpu.VMEM((2, k, wide), F32), pltpu.VMEM((2, k, wide), F32),
             pltpu.VMEM((2, ny, 1, rank), F32), pltpu.VMEM((2, ny, 1, rank), F32),
             pltpu.VMEM((2, nzx, 1, rank + wide), F32), pltpu.VMEM((2, 1, rank + wide), F32),
             pltpu.VMEM((2, ny, 1, rank + wide), F32), pltpu.VMEM((2, 1, rank + wide), F32),
+            pltpu.VMEM((2, nz, k, nx * wide), BF16), pltpu.VMEM((2, k, nx * wide), BF16),
+            pltpu.VMEM((2, nx, k, wide), F32),
             pltpu.VMEM((nzx * nh, 1, wide), F32), pltpu.VMEM((1, wide), F32),
-            dma((6,)), dma((21,)), dma((21,)), dma((3, nz)),
+            dma((6,)), dma((25,)), dma((25,)), dma((5, nz)),
         ],
         compiler_params=pltpu.CompilerParams(collective_id=0, has_side_effects=True),
     )(design_matrix, labels.reshape(1, -1), weights, lambdas.reshape(1, -1), sketch, sketch_values)

time: 110 us -> 108 us (0.982)
  Pallas kernels: 108 us -> 106 us
    pallas_call x1, Pallas kernels: 108 us -> 106 us  [shards(): pl.pallas_call(functools.partial(kernel, sizes), name='step', out_shape=j...]
where the time goes in v3:
time: 108 us
  Pallas kernels  106 us (98%)
  other arithmetic  1.38 us (1%)
    pallas_call x1, Pallas kernels, shards(): pl.pallas_call(functools.partial(kernel, sizes), name='step', out_shape=j...  106 us

profile of v3, /device:TPU:1, one launch (start us, length us, event | category | flops | bytes accessed | tf_op | source)
XLA Modules:
  0.0 107.8 jit_solution(17039421932172125998)
XLA Ops:
  0.0 0.0 copy-start
  0.0 106.4 %step.1 = f32[16,128]{1,0:T(8,128)} custom-call(bf16[128,4096]{1,0:T(8,128)(2,1)} %x_hbm.1, s32[1,128]{1,0:T(1,128)} %bitcast.2, f32[16,64]{1,0:T(8,128)} %w_hbm.1, f32[1,16]{1,0:T(1,128)} %bitcast.3, bf16[64,384]{1,0:T(8,128)(2,1)} %s_hbm.1, f32[384]{0:T(512)} %sv_hbm.1), custom_call_target="tpu_custom_call" | custom-call | tf_op jit(solution)/shard_map/step/pallas_call | solution.py:300
  106.4 0.0 copy-done
  106.4 1.4 %dynamic-slice_add_fusion = f32[16,64]{1,0:T(8,128)} fusion(f32[16,64]{1,0:T(8,128)S(1)} %copy-done, f32[16,128]{1,0:T(8,128)} %step.1, s32[]{:T(128)S(6)} %select_n.3), kind=kLoop, calls=%fused_computation | loop fusion | flops 1024 | bytes 12292 | tf_op jit(solution)/shard_map/add | solution.py:329
Async XLA Ops:
  0.0 106.4 %copy-start = (f32[16,64]{1,0:T(8,128)S(1)}, f32[16,64]{1,0:T(8,128)}, u32[]{:S(2)}) copy-start(f32[16,64]{1,0:T(8,128)} %w_hbm.1) | copy-start | bytes 12292

commit v4 on v3

--- a/solution.py
+++ b/solution.py
@@ -29,7 +29,7 @@
 
 
 def kernel(sizes, x_hbm, labels_hbm, w_hbm, lam_hbm, s_hbm, sv_hbm, out_ref,
-           xv, labels_ref, w_ref, lam_ref, sv_ref, sp, wb, ag, ags, ft, fts, fs, fss, rs0, rss0, rs1, rss1, xr, xs, yh, yhs,
+           xv, labels_ref, w_ref, lam_ref, sv_ref, sp, wb, ag, ags, ft, fts, fs, fss, rs, rss, rl, rls, xr, xs, yh, yhs,
            pr, prs, pz, pzs, pa, pas, cz, czs, cf, kz, kzs, local_sem, send_sem, recv_sem, gather_sem):
     nz, nx, nh, nl, nc = sizes
     nzx, nf, ny = nz * nx, nl * nc, nh * nl * nc
@@ -121,9 +121,11 @@
         start = pl.multiple_of(zz * (nx * wide), nx * wide)
         return lax.dot_general(field, xv[:, pl.ds(start, nx * wide)], BY_LANES, preferred_element_type=F32)
 
-    def gather_rows(i):
+    def gather_rows(i, before_last=None):
         total = jnp.zeros((k, xv.shape[0]), F32)
         for dz in reversed(far_first(nz)):
+            if before_last is not None and dz == nz // 2:
+                before_last()
             arrived_group(2 + i, i, dz, ag.at[i, pl.ds(0, nx if dz else nx - 1)])
             zz = lax.rem(z + (nz - dz), nz)
             total = total + rows_of(jnp.concatenate([ag[i, zz * nx + q] for q in range(nx)], axis=1), zz)
@@ -159,18 +161,26 @@
         whole(8 + i, fs.at[i, pl.ds(0, nf - 1)], f_peers[0][1])
         return jnp.sum(fs[i], axis=0)
 
-    def reduce_columns(i, values, state, scalars):
-        rs, rss = ((rs0, rss0), (rs1, rss1))[i]
+    def reduce_columns(i, values, state, scalars, low_too):
         for dz in far_first(nz):
             zz = lax.rem(z + dz, nz)
             start = pl.multiple_of(zz * (nx * wide), nx * wide)
             part = lax.dot_general(values, xv[:, pl.ds(start, nx * wide)], BY_ROWS, preferred_element_type=F32)
-            rss[zz] = part.astype(rss.dtype)
+            high = part.astype(BF16)
+            rss[i, zz] = high
+            if low_too:
+                rls[zz] = (part - high.astype(F32)).astype(BF16)
             if dz:
-                copy(10 + i, rss.at[zz], rs.at[z], {"samp_0": zz}).start()
-        rs[z] = rss[z]
-        whole(10 + i, rs.at[pl.ds(0, nz - 1)], zx_peers[0][1])
-        along_z = jnp.sum(rs[...].astype(F32), axis=0)
+                copy(10 + i, rss.at[i, zz], rs.at[i, z], {"samp_0": zz}).start()
+        rs[i, z] = rss[i, z]
+        if low_too:
+            for dz in far_first(nz):
+                zz = lax.rem(z + dz, nz)
+                if dz:
+                    copy(25, rls.at[zz], rl.at[z], {"samp_0": zz}).start()
+            rl[z] = rls[z]
+        whole(10 + i, rs.at[i, pl.ds(0, nz - 1)], zx_peers[0][1])
+        along_z = jnp.sum(rs[i].astype(F32), axis=0)
         ridge = (0.5 * lam) * state
         chunks = [along_z[:, q * wide:(q + 1) * wide] + ridge * jnp.where(x == q, 1.0, 0.0) for q in range(nx)]
 
@@ -182,6 +192,10 @@
             copy(14 + i, prs.at[i, j], pr.at[i, y], peer).start()
         pr[i, y] = prs[i, y]
 
+        if low_too:
+            whole(25, rl.at[pl.ds(0, nz - 1)], zx_peers[0][1])
+            low = jnp.sum(rl[...].astype(F32), axis=0)
+            chunks = [chunks[q] + low[:, q * wide:(q + 1) * wide] for q in range(nx)]
         for q in range(nx):
             xs[i, q] = chunks[q]
         for dx in far_first(nx):
@@ -242,25 +256,28 @@
     weights = jnp.where(own, wb[0], wb[1])
     gather_start(0, weights)
     loads[4].wait()
-    for dh in reversed(range(nh)):
-        for dx in far_first(nx):
-            if dh or dx:
-                peer = {"samp_1": lax.rem(x + dx, nx), "samp_2": lax.rem(h + dh, nh)}
-                copy(1, sp.at[x * nh + h], sp.at[x * nh + h], peer).start()
+
+    def sketch_start():
+        for dh in reversed(range(nh)):
+            for dx in far_first(nx):
+                if dh or dx:
+                    peer = {"samp_1": lax.rem(x + dx, nx), "samp_2": lax.rem(h + dh, nh)}
+                    copy(1, sp.at[x * nh + h], sp.at[x * nh + h], peer).start()
+
     loads[5].wait()
 
-    logits = feat_sum(0, gather_rows(0))
+    logits = feat_sum(0, gather_rows(0, sketch_start))
     probability = jax.nn.sigmoid(logits)
     diag = probability * (1.0 - probability)
     miss = (probability - labels_ref[...].astype(F32)).astype(BF16)
     whole(1, sp.at[pl.ds(0, nx * nh - 1)], partner)
     sketch = sp[...].reshape(nx * nh * half, rank)
-    gradient, gradient_pre, image, _ = reduce_columns(0, miss, weights, None)
+    gradient, gradient_pre, image, _ = reduce_columns(0, miss, weights, None, True)
     residual, direction = -gradient, -gradient_pre
     feat_scalars_start(0, pack(0.5 * lanes(residual * direction), 0.5 * lam * lanes(direction * direction)))
     image = -feat_sum(1, spread_rows(0, image))
     scalars = feat_scalars(0) + pack(jnp.zeros((k, 1), F32), lanes(diag * image * image))
-    hess_dir, hess_pre, image_pre, scalars = reduce_columns(1, (diag * image).astype(BF16), direction, scalars)
+    hess_dir, hess_pre, image_pre, scalars = reduce_columns(1, (diag * image).astype(BF16), direction, scalars, False)
     res_dot, curvature = unpack(scalars, 0), unpack(scalars, 1)
     step = res_dot / curvature
     residual = residual - step * hess_dir
@@ -283,7 +300,9 @@
     new_dot, pre_pre, pre_dir = (unpack(scalars, place) for place in range(3))
     beta = new_dot / res_dot
     last = new_dot / (pre_pre + 2.0 * beta * pre_dir + beta * beta * curvature)
-    out_ref[...] = step * direction + last * (precond + beta * direction)
+    update = step * direction + last * (precond + beta * direction)
+    update = jnp.where(h == 0, update, pltpu.roll(update, half, 1))
+    out_ref[...] = w_ref[...] + update[:, :half]
     for arrived in sent:
         arrived.wait_send()
 
@@ -297,10 +316,10 @@
     vmem = pl.BlockSpec(memory_space=pltpu.VMEM)
     anywhere = pl.BlockSpec(memory_space=pl.ANY)
     dma = pltpu.SemaphoreType.DMA
-    update = pl.pallas_call(
+    return pl.pallas_call(
         functools.partial(kernel, sizes),
         name="step",
-        out_shape=jax.ShapeDtypeStruct((k, wide), F32),
+        out_shape=jax.ShapeDtypeStruct((k, half), F32),
         in_specs=[anywhere] * 6,
         out_specs=vmem,
         scratch_shapes=[
@@ -312,7 +331,7 @@
             pltpu.VMEM((3, nzx, k, wide), BF16), pltpu.VMEM((3, k, wide), BF16),
             pltpu.VMEM((3, nf, k, wide), F32), pltpu.VMEM((3, k, wide), F32),
             pltpu.VMEM((2, nf, 1, wide), F32), pltpu.VMEM((2, 1, wide), F32),
-            pltpu.VMEM((nz, k, nx * wide), F32), pltpu.VMEM((nz, k, nx * wide), F32),
+            pltpu.VMEM((2, nz, k, nx * wide), BF16), pltpu.VMEM((2, nz, k, nx * wide), BF16),
             pltpu.VMEM((nz, k, nx * wide), BF16), pltpu.VMEM((nz, k, nx * wide), BF16),
             pltpu.VMEM((2, nx, k, wide), F32), pltpu.VMEM((2, nx, k, wide), F32),
             pltpu.VMEM((2, k, wide), F32), pltpu.VMEM((2, k, wide), F32),
@@ -322,11 +341,10 @@
             pltpu.VMEM((2, nz, k, nx * wide), BF16), pltpu.VMEM((2, k, nx * wide), BF16),
             pltpu.VMEM((2, nx, k, wide), F32),
             pltpu.VMEM((nzx * nh, 1, wide), F32), pltpu.VMEM((1, wide), F32),
-            dma((6,)), dma((25,)), dma((25,)), dma((5, nz)),
+            dma((6,)), dma((26,)), dma((26,)), dma((5, nz)),
         ],
         compiler_params=pltpu.CompilerParams(collective_id=0, has_side_effects=True),
     )(design_matrix, labels.reshape(1, -1), weights, lambdas.reshape(1, -1), sketch, sketch_values)
-    return weights + lax.dynamic_slice_in_dim(update, lax.axis_index("samp_2") * half, half, axis=1)
 
 
 def solution(mesh):

time: 108 us -> 112 us (1.037)
  Pallas kernels: 106 us -> 111 us
  other arithmetic: 1.38 us -> 0 us
  local copies, waits for them, and re-layouts: 0.01 us -> 1.3 us
    pallas_call x1, Pallas kernels: 106 us -> 111 us  [shards(): pl.pallas_call(functools.partial(kernel, sizes), name='step', out_shape=j...]
    add x1 -> x0, other arithmetic: 1.38 us -> none  [shards(): weights + lax.dynamic_slice_in_dim(update, lax.axis_index('samp_2') * hal...]
    unnamed x2 -> x1, local copies, waits for them, and re-layouts: 0.01 us -> 1.3 us
where the time goes in v4:
time: 112 us
  Pallas kernels  111 us (99%)
  local copies, waits for them, and re-layouts  1.3 us (1%)
    pallas_call x1, Pallas kernels, shards(): pl.pallas_call(functools.partial(kernel, sizes), name='step', out_shape=j...  111 us

profile of v4, /device:TPU:1, one launch (start us, length us, event | category | flops | bytes accessed | tf_op | source)
XLA Modules:
  0.0 111.8 jit_solution(237112710067539788)
XLA Ops:
  0.0 110.5 %step.1 = f32[16,64]{1,0:T(8,128)} custom-call(bf16[128,4096]{1,0:T(8,128)(2,1)} %x_hbm.1, s32[1,128]{1,0:T(1,128)} %bitcast.2, f32[16,64]{1,0:T(8,128)} %w_hbm.1, f32[1,16]{1,0:T(1,128)} %bitcast.3, bf16[64,384]{1,0:T(8,128)(2,1)} %s_hbm.1, f32[384]{0:T(512)} %sv_hbm.1), custom_call_target="tpu_custom_call" | custom-call | tf_op jit(solution)/shard_map/step/pallas_call | solution.py:319
  110.5 1.3 %copy.8 = f32[16,64]{1,0:T(8,128)} copy(f32[16,64]{1,0:T(8,128)} %step.1) | data formatting | bytes 8192

commit v5 on v4

--- a/solution.py
+++ b/solution.py
@@ -121,11 +121,9 @@
         start = pl.multiple_of(zz * (nx * wide), nx * wide)
         return lax.dot_general(field, xv[:, pl.ds(start, nx * wide)], BY_LANES, preferred_element_type=F32)
 
-    def gather_rows(i, before_last=None):
+    def gather_rows(i):
         total = jnp.zeros((k, xv.shape[0]), F32)
         for dz in reversed(far_first(nz)):
-            if before_last is not None and dz == nz // 2:
-                before_last()
             arrived_group(2 + i, i, dz, ag.at[i, pl.ds(0, nx if dz else nx - 1)])
             zz = lax.rem(z + (nz - dz), nz)
             total = total + rows_of(jnp.concatenate([ag[i, zz * nx + q] for q in range(nx)], axis=1), zz)
@@ -184,6 +182,9 @@
         ridge = (0.5 * lam) * state
         chunks = [along_z[:, q * wide:(q + 1) * wide] + ridge * jnp.where(x == q, 1.0, 0.0) for q in range(nx)]
 
+        if i == 0:
+            whole(1, sp.at[pl.ds(0, nx * nh - 1)], partner)
+        sketch = sp[...].reshape(nx * nh * half, rank)
         parts = lax.dot_general(split3(jnp.concatenate(chunks, axis=1)), sketch, BY_ROWS, preferred_element_type=F32)
         projected = parts[:k] + parts[k:2 * k] + parts[2 * k:]
         for q in range(k):
@@ -256,22 +257,17 @@
     weights = jnp.where(own, wb[0], wb[1])
     gather_start(0, weights)
     loads[4].wait()
-
-    def sketch_start():
-        for dh in reversed(range(nh)):
-            for dx in far_first(nx):
-                if dh or dx:
-                    peer = {"samp_1": lax.rem(x + dx, nx), "samp_2": lax.rem(h + dh, nh)}
-                    copy(1, sp.at[x * nh + h], sp.at[x * nh + h], peer).start()
-
+    for dh in reversed(range(nh)):
+        for dx in far_first(nx):
+            if dh or dx:
+                peer = {"samp_1": lax.rem(x + dx, nx), "samp_2": lax.rem(h + dh, nh)}
+                copy(1, sp.at[x * nh + h], sp.at[x * nh + h], peer).start()
     loads[5].wait()
 
-    logits = feat_sum(0, gather_rows(0, sketch_start))
+    logits = feat_sum(0, gather_rows(0))
     probability = jax.nn.sigmoid(logits)
     diag = probability * (1.0 - probability)
     miss = (probability - labels_ref[...].astype(F32)).astype(BF16)
-    whole(1, sp.at[pl.ds(0, nx * nh - 1)], partner)
-    sketch = sp[...].reshape(nx * nh * half, rank)
     gradient, gradient_pre, image, _ = reduce_columns(0, miss, weights, None, True)
     residual, direction = -gradient, -gradient_pre
     feat_scalars_start(0, pack(0.5 * lanes(residual * direction), 0.5 * lam * lanes(direction * direction)))

time: 112 us -> 107 us (0.955)
  Pallas kernels: 111 us -> 105 us
    pallas_call x1, Pallas kernels: 111 us -> 105 us  [shards(): pl.pallas_call(functools.partial(kernel, sizes), name='step', out_shape=j...]
where the time goes in v5:
time: 107 us; the launch traced here: 106 us
  Pallas kernels  105 us (98%)
  local copies, waits for them, and re-layouts  1.3 us (1%)
    pallas_call x1, Pallas kernels, shards(): pl.pallas_call(functools.partial(kernel, sizes), name='step', out_shape=j...  105 us

profile of v5, /device:TPU:1, one launch (start us, length us, event | category | flops | bytes accessed | tf_op | source)
XLA Modules:
  0.0 106.4 jit_solution(6193768796596688414)
XLA Ops:
  0.0 105.1 %step.1 = f32[16,64]{1,0:T(8,128)} custom-call(bf16[128,4096]{1,0:T(8,128)(2,1)} %x_hbm.1, s32[1,128]{1,0:T(1,128)} %bitcast.2, f32[16,64]{1,0:T(8,128)} %w_hbm.1, f32[1,16]{1,0:T(1,128)} %bitcast.3, bf16[64,384]{1,0:T(8,128)(2,1)} %s_hbm.1, f32[384]{0:T(512)} %sv_hbm.1), custom_call_target="tpu_custom_call" | custom-call | tf_op jit(solution)/shard_map/step/pallas_call | solution.py:315
  105.1 1.3 %copy.8 = f32[16,64]{1,0:T(8,128)} copy(f32[16,64]{1,0:T(8,128)} %step.1) | data formatting | bytes 8192

commit v6 on v3

--- a/solution.py
+++ b/solution.py
@@ -29,8 +29,8 @@
 
 
 def kernel(sizes, x_hbm, labels_hbm, w_hbm, lam_hbm, s_hbm, sv_hbm, out_ref,
-           xv, labels_ref, w_ref, lam_ref, sv_ref, sp, wb, ag, ags, ft, fts, fs, fss, rs0, rss0, rs1, rss1, xr, xs, yh, yhs,
-           pr, prs, pz, pzs, pa, pas, cz, czs, cf, kz, kzs, local_sem, send_sem, recv_sem, gather_sem):
+           xv, labels_ref, w_ref, lam_ref, sv_ref, sp, wb, ag, ags, ft, fts, fs, fss, rs, rss, rl, rls, ws, wss, xr, xs, zr, zs, spz, yh, yhs,
+           pr, prs, pz, pzs, pa, pas, cz, czs, cf, dz_ref, dzs, df, kz, kzs, local_sem, send_sem, recv_sem, gather_sem, ring_sem):
     nz, nx, nh, nl, nc = sizes
     nzx, nf, ny = nz * nx, nl * nc, nh * nl * nc
     k, half = w_ref.shape
@@ -103,13 +103,13 @@
                         src_ref=ags.at[i], dst_ref=ag.at[i, zx], send_sem=send_sem.at[2 + i], recv_sem=gather_sem.at[i, dz],
                         device_id={"samp_0": zz, "samp_1": xx}, device_id_type=pl.DeviceIdType.MESH).start()
 
-    def spread_start(i, value):
-        czs[i] = value.astype(BF16)
+    def spread_start(value):
+        czs[...] = value.astype(BF16)
         for dz in far_first(nz):
             zz = lax.rem(z + dz, nz)
             if dz:
                 pltpu.make_async_remote_copy(
-                    src_ref=czs.at[i], dst_ref=cz.at[i, z], send_sem=send_sem.at[23 + i], recv_sem=gather_sem.at[3 + i, dz],
+                    src_ref=czs, dst_ref=cz.at[z], send_sem=send_sem.at[23], recv_sem=gather_sem.at[3, dz],
                     device_id={"samp_0": zz}, device_id_type=pl.DeviceIdType.MESH).start()
 
     def arrived_group(phase, place, dz, group):
@@ -130,22 +130,51 @@
         sent.append(copy(2 + i, ag.at[i, pl.ds(0, nzx - 1)], ag.at[i, pl.ds(0, nzx - 1)], zx_peers[0][1]))
         return total
 
-    def spread_rows(i, total):
+    def spread_rows(total):
         for dz in reversed(far_first(nz)):
             zz = lax.rem(z + (nz - dz), nz)
             if dz:
-                arrived_group(23 + i, 3 + i, dz, cz.at[i, 0])
-                total = total + rows_of(cz[i, zz], zz)
+                arrived_group(23, 3, dz, cz.at[0])
+                total = total + rows_of(cz[zz], zz)
             else:
-                total = total + rows_of(czs[i], zz)
-        sent.append(copy(23 + i, cz.at[i, pl.ds(0, nz - 1)], cz.at[i, pl.ds(0, nz - 1)], zx_peers[0][1]))
+                total = total + rows_of(czs[...], zz)
+        sent.append(copy(23, cz.at[pl.ds(0, nz - 1)], cz.at[pl.ds(0, nz - 1)], zx_peers[0][1]))
         return total
 
-    def feat_sum(i, value):
+    def x_spread_rows(total):
+        whole(24, dz_ref.at[pl.ds(0, nx - 1)], {"samp_1": lax.rem(x + 1, nx)})
+        for zz in range(nz):
+            field = jnp.concatenate([dz_ref[q, :, zz * wide:(zz + 1) * wide] for q in range(nx)], axis=1)
+            total = total + rows_of(field, zz)
+        return total
+
+    def ring(step):
+        ahead, behind = {"samp_0": lax.rem(z + 1, nz)}, {"samp_0": lax.rem(z + nz - 1, nz)}
+        for way, peer in ((0, ahead), (1, behind)):
+            if step > 1 and (way == 0 or step <= nz // 2):
+                last = spz.at[0]
+                pltpu.make_async_remote_copy(
+                    src_ref=last, dst_ref=last, send_sem=send_sem.at[26], recv_sem=ring_sem.at[step - 2, way],
+                    device_id=peer, device_id_type=pl.DeviceIdType.MESH).wait_recv()
+            if step <= nz // 2 - way:
+                offset = step - 1 if way else nz - (step - 1)
+                block = lax.rem(z + offset, nz)
+                pltpu.make_async_remote_copy(
+                    src_ref=sp.at[pl.ds(x * nh, nh)] if step == 1 else spz.at[block], dst_ref=spz.at[block],
+                    send_sem=send_sem.at[26], recv_sem=ring_sem.at[step - 1, way],
+                    device_id=peer, device_id_type=pl.DeviceIdType.MESH).start()
+        if step == 1:
+            spz[z] = sp[pl.ds(x * nh, nh)]
+        if step == nz // 2 + 1:
+            sent.append(copy(26, spz.at[pl.ds(0, nz - 1)], spz.at[pl.ds(0, nz - 1)], ahead))
+
+    def feat_sum(i, value, step=None):
         fts[i] = value
         ft[i, f] = value
         for _, peer in f_peers:
             copy(5 + i, fts.at[i], ft.at[i, f], peer).start()
+        if step:
+            ring(step)
         whole(5 + i, ft.at[i, pl.ds(0, nf - 1)], f_peers[0][1])
         return jnp.sum(ft[i], axis=0)
 
@@ -159,21 +188,87 @@
         whole(8 + i, fs.at[i, pl.ds(0, nf - 1)], f_peers[0][1])
         return jnp.sum(fs[i], axis=0)
 
-    def reduce_columns(i, values, state, scalars):
-        rs, rss = ((rs0, rss0), (rs1, rss1))[i]
+    def along_z(values, state):
         for dz in far_first(nz):
             zz = lax.rem(z + dz, nz)
             start = pl.multiple_of(zz * (nx * wide), nx * wide)
             part = lax.dot_general(values, xv[:, pl.ds(start, nx * wide)], BY_ROWS, preferred_element_type=F32)
-            rss[zz] = part.astype(rss.dtype)
+            high = part.astype(BF16)
+            rss[zz] = high
+            rls[zz] = (part - high.astype(F32)).astype(BF16)
             if dz:
-                copy(10 + i, rss.at[zz], rs.at[z], {"samp_0": zz}).start()
+                copy(10, rss.at[zz], rs.at[z], {"samp_0": zz}).start()
         rs[z] = rss[z]
-        whole(10 + i, rs.at[pl.ds(0, nz - 1)], zx_peers[0][1])
-        along_z = jnp.sum(rs[...].astype(F32), axis=0)
+        for dz in far_first(nz):
+            zz = lax.rem(z + dz, nz)
+            if dz:
+                copy(25, rls.at[zz], rl.at[z], {"samp_0": zz}).start()
+        rl[z] = rls[z]
+        whole(10, rs.at[pl.ds(0, nz - 1)], zx_peers[0][1])
+        total = jnp.sum(rs[...].astype(F32), axis=0)
         ridge = (0.5 * lam) * state
-        chunks = [along_z[:, q * wide:(q + 1) * wide] + ridge * jnp.where(x == q, 1.0, 0.0) for q in range(nx)]
-
+        chunks = [total[:, q * wide:(q + 1) * wide] + ridge * jnp.where(x == q, 1.0, 0.0) for q in range(nx)]
+        whole(1, sp.at[pl.ds(0, nx * nh - 1)], partner)
+        sketch = sp[...].reshape(nx * nh * half, rank)
+        project_start(0, chunks, sketch)
+        ring(1)
+
+        whole(25, rl.at[pl.ds(0, nz - 1)], zx_peers[0][1])
+        low = jnp.sum(rl[...].astype(F32), axis=0)
+        for q in range(nx):
+            xs[q] = chunks[q] + low[:, q * wide:(q + 1) * wide]
+        for dx in far_first(nx):
+            xx = lax.rem(x + dx, nx)
+            if dx:
+                copy(21, xs.at[xx], xr.at[x], {"samp_1": xx}).start()
+        xr[x] = xs[x]
+        whole(21, xr.at[pl.ds(0, nx - 1)], {"samp_1": lax.rem(x + 1, nx)})
+        vector, image, full = project_finish(0, jnp.sum(xr[...], axis=0), None, 2)
+        correction = spread(full, sketch)
+        spread_start(correction)
+        for q in range(nx):
+            cf[q] = correction[:, q * wide:(q + 1) * wide]
+        return vector, vector + cf[x], image
+
+    def along_x(values, state, scalars):
+        for zz in range(nz):
+            part = lax.dot_general(values, xv[:, zz * nx * wide:(zz + 1) * nx * wide], BY_ROWS, preferred_element_type=F32)
+            for q in range(nx):
+                wss[q, :, zz * wide:(zz + 1) * wide] = part[:, q * wide:(q + 1) * wide].astype(BF16)
+        for dx in far_first(nx):
+            xx = lax.rem(x + dx, nx)
+            if dx:
+                copy(11, wss.at[xx], ws.at[x], {"samp_1": xx}).start()
+        ws[x] = wss[x]
+        ring(4)
+        whole(11, ws.at[pl.ds(0, nx - 1)], {"samp_1": lax.rem(x + 1, nx)})
+        total = jnp.sum(ws[...].astype(F32), axis=0)
+        ridge = (0.5 * lam) * state
+        chunks = [total[:, q * wide:(q + 1) * wide] + ridge * jnp.where(z == q, 1.0, 0.0) for q in range(nz)]
+        ring(5)
+        sketch = spz[...].reshape(nz * nh * half, rank)
+        project_start(1, chunks, sketch)
+
+        for q in range(nz):
+            zs[q] = chunks[q]
+        for dz in far_first(nz):
+            zz = lax.rem(z + dz, nz)
+            if dz:
+                copy(22, zs.at[zz], zr.at[z], {"samp_0": zz}).start()
+        zr[z] = zs[z]
+        whole(22, zr.at[pl.ds(0, nz - 1)], zx_peers[0][1])
+        vector, image, full = project_finish(1, jnp.sum(zr[...], axis=0), scalars, None)
+        correction = spread(full, sketch)
+        dzs[...] = correction.astype(BF16)
+        for dx in far_first(nx):
+            if dx:
+                copy(24, dzs, dz_ref.at[x], {"samp_1": lax.rem(x + dx, nx)}).start()
+        dz_ref[x] = dzs[...]
+        for q in range(nz):
+            df[q] = correction[:, q * wide:(q + 1) * wide]
+        return vector, vector + df[z], image, jnp.sum(full[:, rank:], axis=0, keepdims=True) * (1.0 / nf)
+
+    def project_start(i, chunks, sketch):
         parts = lax.dot_general(split3(jnp.concatenate(chunks, axis=1)), sketch, BY_ROWS, preferred_element_type=F32)
         projected = parts[:k] + parts[k:2 * k] + parts[2 * k:]
         for q in range(k):
@@ -182,15 +277,11 @@
             copy(14 + i, prs.at[i, j], pr.at[i, y], peer).start()
         pr[i, y] = prs[i, y]
 
-        for q in range(nx):
-            xs[i, q] = chunks[q]
-        for dx in far_first(nx):
-            xx = lax.rem(x + dx, nx)
-            if dx:
-                copy(21 + i, xs.at[i, xx], xr.at[i, x], {"samp_1": xx}).start()
-        xr[i, x] = xs[i, x]
-        whole(21 + i, xr.at[i, pl.ds(0, nx - 1)], {"samp_1": lax.rem(x + 1, nx)})
-        part = jnp.sum(xr[i], axis=0)
+    def spread(full, sketch):
+        parts = lax.dot_general(split3(ratios * full[:, :rank]), sketch, BY_LANES, preferred_element_type=F32)
+        return parts[:k] + parts[k:2 * k] + parts[2 * k:]
+
+    def project_finish(i, part, scalars, step):
         yhs[i] = part
         copy(12 + i, yhs.at[i], yh.at[i], partner).start()
 
@@ -214,18 +305,11 @@
         pa[i, y, :, across] = mine
         for _, peer in y_peers:
             copy(18 + i, pas.at[i, :, across], pa.at[i, y, :, across], peer).start()
+        if step:
+            ring(step)
         image = gather_rows(1 + i)
         whole(18 + i, pa.at[i, pl.ds(0, ny - 1), :, across], y_peers[0][1])
-        full = jnp.concatenate([pa[i, q, :, across] for q in range(k)], axis=0)
-        if scalars is not None:
-            scalars = jnp.sum(full[:, rank:], axis=0, keepdims=True) * (1.0 / nf)
-
-        parts = lax.dot_general(split3(ratios * full[:, :rank]), sketch, BY_LANES, preferred_element_type=F32)
-        correction = parts[:k] + parts[k:2 * k] + parts[2 * k:]
-        spread_start(i, correction)
-        for q in range(nx):
-            cf[i, q] = correction[:, q * wide:(q + 1) * wide]
-        return vector, vector + cf[i, x], image, scalars
+        return vector, image, jnp.concatenate([pa[i, q, :, across] for q in range(k)], axis=0)
 
     for load in loads[:4]:
         load.wait()
@@ -253,21 +337,19 @@
     probability = jax.nn.sigmoid(logits)
     diag = probability * (1.0 - probability)
     miss = (probability - labels_ref[...].astype(F32)).astype(BF16)
-    whole(1, sp.at[pl.ds(0, nx * nh - 1)], partner)
-    sketch = sp[...].reshape(nx * nh * half, rank)
-    gradient, gradient_pre, image, _ = reduce_columns(0, miss, weights, None)
+    gradient, gradient_pre, image = along_z(miss, weights)
     residual, direction = -gradient, -gradient_pre
     feat_scalars_start(0, pack(0.5 * lanes(residual * direction), 0.5 * lam * lanes(direction * direction)))
-    image = -feat_sum(1, spread_rows(0, image))
+    image = -feat_sum(1, spread_rows(image), 3)
     scalars = feat_scalars(0) + pack(jnp.zeros((k, 1), F32), lanes(diag * image * image))
-    hess_dir, hess_pre, image_pre, scalars = reduce_columns(1, (diag * image).astype(BF16), direction, scalars)
+    hess_dir, hess_pre, image_pre, scalars = along_x((diag * image).astype(BF16), direction, scalars)
     res_dot, curvature = unpack(scalars, 0), unpack(scalars, 1)
     step = res_dot / curvature
     residual = residual - step * hess_dir
     precond = direction - step * hess_pre
     feat_scalars_start(1, pack(0.5 * lanes(residual * precond), 0.5 * lam * lanes(precond * precond),
                                0.5 * lam * lanes(precond * direction)))
-    image_pre = image - step * feat_sum(2, spread_rows(1, image_pre))
+    image_pre = image - step * feat_sum(2, x_spread_rows(image_pre))
     mine = feat_scalars(1) + pack(jnp.zeros((k, 1), F32), lanes(diag * image_pre * image_pre),
                                   lanes(diag * image_pre * image))
     kzs[...] = mine
@@ -283,7 +365,9 @@
     new_dot, pre_pre, pre_dir = (unpack(scalars, place) for place in range(3))
     beta = new_dot / res_dot
     last = new_dot / (pre_pre + 2.0 * beta * pre_dir + beta * beta * curvature)
-    out_ref[...] = step * direction + last * (precond + beta * direction)
+    update = step * direction + last * (precond + beta * direction)
+    update = jnp.where(h == 0, update, pltpu.roll(update, half, 1))
+    out_ref[...] = w_ref[...] + update[:, :half]
     for arrived in sent:
         arrived.wait_send()
 
@@ -297,10 +381,10 @@
     vmem = pl.BlockSpec(memory_space=pltpu.VMEM)
     anywhere = pl.BlockSpec(memory_space=pl.ANY)
     dma = pltpu.SemaphoreType.DMA
-    update = pl.pallas_call(
+    return pl.pallas_call(
         functools.partial(kernel, sizes),
         name="step",
-        out_shape=jax.ShapeDtypeStruct((k, wide), F32),
+        out_shape=jax.ShapeDtypeStruct((k, half), F32),
         in_specs=[anywhere] * 6,
         out_specs=vmem,
         scratch_shapes=[
@@ -312,21 +396,25 @@
             pltpu.VMEM((3, nzx, k, wide), BF16), pltpu.VMEM((3, k, wide), BF16),
             pltpu.VMEM((3, nf, k, wide), F32), pltpu.VMEM((3, k, wide), F32),
             pltpu.VMEM((2, nf, 1, wide), F32), pltpu.VMEM((2, 1, wide), F32),
-            pltpu.VMEM((nz, k, nx * wide), F32), pltpu.VMEM((nz, k, nx * wide), F32),
             pltpu.VMEM((nz, k, nx * wide), BF16), pltpu.VMEM((nz, k, nx * wide), BF16),
-            pltpu.VMEM((2, nx, k, wide), F32), pltpu.VMEM((2, nx, k, wide), F32),
+            pltpu.VMEM((nz, k, nx * wide), BF16), pltpu.VMEM((nz, k, nx * wide), BF16),
+            pltpu.VMEM((nx, k, nz * wide), BF16), pltpu.VMEM((nx, k, nz * wide), BF16),
+            pltpu.VMEM((nx, k, wide), F32), pltpu.VMEM((nx, k, wide), F32),
+            pltpu.VMEM((nz, k, wide), F32), pltpu.VMEM((nz, k, wide), F32),
+            pltpu.VMEM((nz, nh, half, rank), BF16),
             pltpu.VMEM((2, k, wide), F32), pltpu.VMEM((2, k, wide), F32),
             pltpu.VMEM((2, ny, 1, rank), F32), pltpu.VMEM((2, ny, 1, rank), F32),
             pltpu.VMEM((2, nzx, 1, rank + wide), F32), pltpu.VMEM((2, 1, rank + wide), F32),
             pltpu.VMEM((2, ny, 1, rank + wide), F32), pltpu.VMEM((2, 1, rank + wide), F32),
-            pltpu.VMEM((2, nz, k, nx * wide), BF16), pltpu.VMEM((2, k, nx * wide), BF16),
-            pltpu.VMEM((2, nx, k, wide), F32),
+            pltpu.VMEM((nz, k, nx * wide), BF16), pltpu.VMEM((k, nx * wide), BF16),
+            pltpu.VMEM((nx, k, wide), F32),
+            pltpu.VMEM((nx, k, nz * wide), BF16), pltpu.VMEM((k, nz * wide), BF16),
+            pltpu.VMEM((nz, k, wide), F32),
             pltpu.VMEM((nzx * nh, 1, wide), F32), pltpu.VMEM((1, wide), F32),
-            dma((6,)), dma((25,)), dma((25,)), dma((5, nz)),
+            dma((6,)), dma((27,)), dma((27,)), dma((4, nz)), dma((nz // 2, 2)),
         ],
         compiler_params=pltpu.CompilerParams(collective_id=0, has_side_effects=True),
     )(design_matrix, labels.reshape(1, -1), weights, lambdas.reshape(1, -1), sketch, sketch_values)
-    return weights + lax.dynamic_slice_in_dim(update, lax.axis_index("samp_2") * half, half, axis=1)
 
 
 def solution(mesh):

time: 108 us -> 104 us (0.963)
  Pallas kernels: 106 us -> 103 us
  other arithmetic: 1.38 us -> 0 us
  local copies, waits for them, and re-layouts: 0.01 us -> 1.3 us
    pallas_call x1, Pallas kernels: 106 us -> 103 us  [shards(): pl.pallas_call(functools.partial(kernel, sizes), name='step', out_shape=j...]
    add x1 -> x0, other arithmetic: 1.38 us -> none  [shards(): weights + lax.dynamic_slice_in_dim(update, lax.axis_index('samp_2') * hal...]
    unnamed x2 -> x1, local copies, waits for them, and re-layouts: 0.01 us -> 1.3 us
where the time goes in v6:
time: 104 us
  Pallas kernels  103 us (99%)
  local copies, waits for them, and re-layouts  1.3 us (1%)
    pallas_call x1, Pallas kernels, shards(): pl.pallas_call(functools.partial(kernel, sizes), name='step', out_shape=j...  103 us

profile of v6, /device:TPU:1, one launch (start us, length us, event | category | flops | bytes accessed | tf_op | source)
XLA Modules:
  0.0 104.1 jit_solution(8022963363106578871)
XLA Ops:
  0.0 102.8 %step.1 = f32[16,64]{1,0:T(8,128)} custom-call(bf16[128,4096]{1,0:T(8,128)(2,1)} %x_hbm.1, s32[1,128]{1,0:T(1,128)} %bitcast.2, f32[16,64]{1,0:T(8,128)} %w_hbm.1, f32[1,16]{1,0:T(1,128)} %bitcast.3, bf16[64,384]{1,0:T(8,128)(2,1)} %s_hbm.1, f32[384]{0:T(512)} %sv_hbm.1), custom_call_target="tpu_custom_call" | custom-call | tf_op jit(solution)/shard_map/step/pallas_call | solution.py:384
  102.8 1.3 %copy.8 = f32[16,64]{1,0:T(8,128)} copy(f32[16,64]{1,0:T(8,128)} %step.1) | data formatting | bytes 8192

commit v7 on v6

--- a/solution.py
+++ b/solution.py
@@ -29,8 +29,8 @@
 
 
 def kernel(sizes, x_hbm, labels_hbm, w_hbm, lam_hbm, s_hbm, sv_hbm, out_ref,
-           xv, labels_ref, w_ref, lam_ref, sv_ref, sp, wb, ag, ags, ft, fts, fs, fss, rs, rss, rl, rls, ws, wss, xr, xs, zr, zs, spz, yh, yhs,
-           pr, prs, pz, pzs, pa, pas, cz, czs, cf, dz_ref, dzs, df, kz, kzs, local_sem, send_sem, recv_sem, gather_sem, ring_sem):
+           xv, xw, labels_ref, w_ref, lam_ref, sv_ref, sp, wb, ag, ags, ft, fts, fs, fss, rs, rss, rl, rls, ws, wss, xr, xs, zr, zs, spz, yh, yhs,
+           pr, prs, pz, pzs, pa, pas, cx, cxs, cf, kz, kzs, local_sem, send_sem, recv_sem, gather_sem, ring_sem, x_sem):
     nz, nx, nh, nl, nc = sizes
     nzx, nf, ny = nz * nx, nl * nc, nh * nl * nc
     k, half = w_ref.shape
@@ -64,6 +64,10 @@
         [(w_hbm, w_ref), (lam_hbm, lam_ref), (sv_hbm, sv_ref), (labels_hbm, labels_ref), (s_hbm, sp.at[x * nh + h]), (x_hbm, xv)])]
     for load in loads:
         load.start()
+    for q in range(nx):
+        for zz in range(nz):
+            pltpu.make_async_copy(x_hbm.at[:, pl.ds((zz * nx + q) * wide, wide)], xw.at[:, pl.ds((q * nz + zz) * wide, wide)],
+                                  local_sem.at[6]).start()
 
     def copy(phase, src, dst, peer):
         return pltpu.make_async_remote_copy(
@@ -103,15 +107,6 @@
                         src_ref=ags.at[i], dst_ref=ag.at[i, zx], send_sem=send_sem.at[2 + i], recv_sem=gather_sem.at[i, dz],
                         device_id={"samp_0": zz, "samp_1": xx}, device_id_type=pl.DeviceIdType.MESH).start()
 
-    def spread_start(value):
-        czs[...] = value.astype(BF16)
-        for dz in far_first(nz):
-            zz = lax.rem(z + dz, nz)
-            if dz:
-                pltpu.make_async_remote_copy(
-                    src_ref=czs, dst_ref=cz.at[z], send_sem=send_sem.at[23], recv_sem=gather_sem.at[3, dz],
-                    device_id={"samp_0": zz}, device_id_type=pl.DeviceIdType.MESH).start()
-
     def arrived_group(phase, place, dz, group):
         pltpu.make_async_remote_copy(
             src_ref=group, dst_ref=group, send_sem=send_sem.at[phase], recv_sem=gather_sem.at[place, dz],
@@ -130,22 +125,31 @@
         sent.append(copy(2 + i, ag.at[i, pl.ds(0, nzx - 1)], ag.at[i, pl.ds(0, nzx - 1)], zx_peers[0][1]))
         return total
 
-    def spread_rows(total):
-        for dz in reversed(far_first(nz)):
-            zz = lax.rem(z + (nz - dz), nz)
-            if dz:
-                arrived_group(23, 3, dz, cz.at[0])
-                total = total + rows_of(cz[zz], zz)
+    def by_x(xx):
+        return pl.ds(pl.multiple_of(xx * (nz * wide), nz * wide), nz * wide)
+
+    def spread_start(i, value):
+        cxs[i] = value.astype(BF16)
+        for dx in far_first(nx):
+            if dx:
+                pltpu.make_async_remote_copy(
+                    src_ref=cxs.at[i], dst_ref=cx.at[i, x], send_sem=send_sem.at[23 + i], recv_sem=x_sem.at[i, dx],
+                    device_id={"samp_1": lax.rem(x + dx, nx)}, device_id_type=pl.DeviceIdType.MESH).start()
+        for q in range(nz):
+            cf[q] = value[:, q * wide:(q + 1) * wide]
+
+    def spread_rows(i, total):
+        for dx in reversed(far_first(nx)):
+            xx = lax.rem(x + (nx - dx), nx)
+            if dx:
+                pltpu.make_async_remote_copy(
+                    src_ref=cxs.at[i], dst_ref=cx.at[i, xx], send_sem=send_sem.at[23 + i], recv_sem=x_sem.at[i, dx],
+                    device_id={"samp_1": xx}, device_id_type=pl.DeviceIdType.MESH).wait_recv()
+                field = cx[i, xx]
             else:
-                total = total + rows_of(czs[...], zz)
-        sent.append(copy(23, cz.at[pl.ds(0, nz - 1)], cz.at[pl.ds(0, nz - 1)], zx_peers[0][1]))
-        return total
-
-    def x_spread_rows(total):
-        whole(24, dz_ref.at[pl.ds(0, nx - 1)], {"samp_1": lax.rem(x + 1, nx)})
-        for zz in range(nz):
-            field = jnp.concatenate([dz_ref[q, :, zz * wide:(zz + 1) * wide] for q in range(nx)], axis=1)
-            total = total + rows_of(field, zz)
+                field = cxs[i]
+            total = total + lax.dot_general(field, xw[:, by_x(xx)], BY_LANES, preferred_element_type=F32)
+        sent.append(copy(23 + i, cx.at[i, pl.ds(0, nx - 1)], cx.at[i, pl.ds(0, nx - 1)], zx_peers[0][1]))
         return total
 
     def ring(step):
@@ -168,13 +172,14 @@
         if step == nz // 2 + 1:
             sent.append(copy(26, spz.at[pl.ds(0, nz - 1)], spz.at[pl.ds(0, nz - 1)], ahead))
 
-    def feat_sum(i, value, step=None):
+    def feat_sum(i, value):
         fts[i] = value
         ft[i, f] = value
         for _, peer in f_peers:
             copy(5 + i, fts.at[i], ft.at[i, f], peer).start()
-        if step:
-            ring(step)
+        if i == 0:
+            whole(27, sp.at[x * nh + 1 - h], partner)
+            ring(1)
         whole(5 + i, ft.at[i, pl.ds(0, nf - 1)], f_peers[0][1])
         return jnp.sum(ft[i], axis=0)
 
@@ -208,10 +213,9 @@
         total = jnp.sum(rs[...].astype(F32), axis=0)
         ridge = (0.5 * lam) * state
         chunks = [total[:, q * wide:(q + 1) * wide] + ridge * jnp.where(x == q, 1.0, 0.0) for q in range(nx)]
-        whole(1, sp.at[pl.ds(0, nx * nh - 1)], partner)
-        sketch = sp[...].reshape(nx * nh * half, rank)
-        project_start(0, chunks, sketch)
-        ring(1)
+        whole(1, sp.at[pl.ds(0, (nx - 1) * nh)], partner)
+        project_start(0, chunks, sp[...].reshape(nx * nh * half, rank))
+        ring(2)
 
         whole(25, rl.at[pl.ds(0, nz - 1)], zx_peers[0][1])
         low = jnp.sum(rl[...].astype(F32), axis=0)
@@ -223,31 +227,24 @@
                 copy(21, xs.at[xx], xr.at[x], {"samp_1": xx}).start()
         xr[x] = xs[x]
         whole(21, xr.at[pl.ds(0, nx - 1)], {"samp_1": lax.rem(x + 1, nx)})
-        vector, image, full = project_finish(0, jnp.sum(xr[...], axis=0), None, 2)
-        correction = spread(full, sketch)
-        spread_start(correction)
-        for q in range(nx):
-            cf[q] = correction[:, q * wide:(q + 1) * wide]
-        return vector, vector + cf[x], image
+        vector, image, full = project_finish(0, jnp.sum(xr[...], axis=0), None)
+        ring(5)
+        spread_start(0, spread(full))
+        return vector, vector + cf[z], image
 
     def along_x(values, state, scalars):
-        for zz in range(nz):
-            part = lax.dot_general(values, xv[:, zz * nx * wide:(zz + 1) * nx * wide], BY_ROWS, preferred_element_type=F32)
-            for q in range(nx):
-                wss[q, :, zz * wide:(zz + 1) * wide] = part[:, q * wide:(q + 1) * wide].astype(BF16)
         for dx in far_first(nx):
             xx = lax.rem(x + dx, nx)
+            part = lax.dot_general(values, xw[:, by_x(xx)], BY_ROWS, preferred_element_type=F32)
+            wss[xx] = part.astype(BF16)
             if dx:
                 copy(11, wss.at[xx], ws.at[x], {"samp_1": xx}).start()
         ws[x] = wss[x]
-        ring(4)
         whole(11, ws.at[pl.ds(0, nx - 1)], {"samp_1": lax.rem(x + 1, nx)})
         total = jnp.sum(ws[...].astype(F32), axis=0)
         ridge = (0.5 * lam) * state
         chunks = [total[:, q * wide:(q + 1) * wide] + ridge * jnp.where(z == q, 1.0, 0.0) for q in range(nz)]
-        ring(5)
-        sketch = spz[...].reshape(nz * nh * half, rank)
-        project_start(1, chunks, sketch)
+        project_start(1, chunks, spz[...].reshape(nz * nh * half, rank))
 
         for q in range(nz):
             zs[q] = chunks[q]
@@ -257,16 +254,9 @@
                 copy(22, zs.at[zz], zr.at[z], {"samp_0": zz}).start()
         zr[z] = zs[z]
         whole(22, zr.at[pl.ds(0, nz - 1)], zx_peers[0][1])
-        vector, image, full = project_finish(1, jnp.sum(zr[...], axis=0), scalars, None)
-        correction = spread(full, sketch)
-        dzs[...] = correction.astype(BF16)
-        for dx in far_first(nx):
-            if dx:
-                copy(24, dzs, dz_ref.at[x], {"samp_1": lax.rem(x + dx, nx)}).start()
-        dz_ref[x] = dzs[...]
-        for q in range(nz):
-            df[q] = correction[:, q * wide:(q + 1) * wide]
-        return vector, vector + df[z], image, jnp.sum(full[:, rank:], axis=0, keepdims=True) * (1.0 / nf)
+        vector, image, full = project_finish(1, jnp.sum(zr[...], axis=0), scalars)
+        spread_start(1, spread(full))
+        return vector, vector + cf[z], image, jnp.sum(full[:, rank:], axis=0, keepdims=True) * (1.0 / nf)
 
     def project_start(i, chunks, sketch):
         parts = lax.dot_general(split3(jnp.concatenate(chunks, axis=1)), sketch, BY_ROWS, preferred_element_type=F32)
@@ -277,11 +267,12 @@
             copy(14 + i, prs.at[i, j], pr.at[i, y], peer).start()
         pr[i, y] = prs[i, y]
 
-    def spread(full, sketch):
+    def spread(full):
+        sketch = spz[...].reshape(nz * nh * half, rank)
         parts = lax.dot_general(split3(ratios * full[:, :rank]), sketch, BY_LANES, preferred_element_type=F32)
         return parts[:k] + parts[k:2 * k] + parts[2 * k:]
 
-    def project_finish(i, part, scalars, step):
+    def project_finish(i, part, scalars):
         yhs[i] = part
         copy(12 + i, yhs.at[i], yh.at[i], partner).start()
 
@@ -294,6 +285,8 @@
         pz[i, zx, :, across] = mine
         for _, peer in zx_peers:
             copy(16 + i, pzs.at[i, :, across], pz.at[i, zx, :, across], peer).start()
+        if i == 0:
+            ring(3)
 
         whole(12 + i, yh.at[i], partner)
         vector = part + yh[i]
@@ -305,8 +298,8 @@
         pa[i, y, :, across] = mine
         for _, peer in y_peers:
             copy(18 + i, pas.at[i, :, across], pa.at[i, y, :, across], peer).start()
-        if step:
-            ring(step)
+        if i == 0:
+            ring(4)
         image = gather_rows(1 + i)
         whole(18 + i, pa.at[i, pl.ds(0, ny - 1), :, across], y_peers[0][1])
         return vector, image, jnp.concatenate([pa[i, q, :, across] for q in range(k)], axis=0)
@@ -321,17 +314,19 @@
     wb[0, :, half:] = w_ref[...]
     pl.semaphore_wait(barrier, len(zx_peers) + len(y_peers))
     copy(0, wb.at[0], wb.at[1], partner).start()
+    loads[4].wait()
+    copy(27, sp.at[x * nh + h], sp.at[x * nh + h], partner).start()
     whole(0, wb.at[1], partner)
     own = (lane // half) == h
     weights = jnp.where(own, wb[0], wb[1])
     gather_start(0, weights)
-    loads[4].wait()
     for dh in reversed(range(nh)):
         for dx in far_first(nx):
-            if dh or dx:
+            if dx:
                 peer = {"samp_1": lax.rem(x + dx, nx), "samp_2": lax.rem(h + dh, nh)}
                 copy(1, sp.at[x * nh + h], sp.at[x * nh + h], peer).start()
     loads[5].wait()
+    pltpu.make_async_copy(x_hbm, xw, local_sem.at[6]).wait()
 
     logits = feat_sum(0, gather_rows(0))
     probability = jax.nn.sigmoid(logits)
@@ -340,7 +335,7 @@
     gradient, gradient_pre, image = along_z(miss, weights)
     residual, direction = -gradient, -gradient_pre
     feat_scalars_start(0, pack(0.5 * lanes(residual * direction), 0.5 * lam * lanes(direction * direction)))
-    image = -feat_sum(1, spread_rows(image), 3)
+    image = -feat_sum(1, spread_rows(0, image))
     scalars = feat_scalars(0) + pack(jnp.zeros((k, 1), F32), lanes(diag * image * image))
     hess_dir, hess_pre, image_pre, scalars = along_x((diag * image).astype(BF16), direction, scalars)
     res_dot, curvature = unpack(scalars, 0), unpack(scalars, 1)
@@ -349,7 +344,7 @@
     precond = direction - step * hess_pre
     feat_scalars_start(1, pack(0.5 * lanes(residual * precond), 0.5 * lam * lanes(precond * precond),
                                0.5 * lam * lanes(precond * direction)))
-    image_pre = image - step * feat_sum(2, x_spread_rows(image_pre))
+    image_pre = image - step * feat_sum(2, spread_rows(1, image_pre))
     mine = feat_scalars(1) + pack(jnp.zeros((k, 1), F32), lanes(diag * image_pre * image_pre),
                                   lanes(diag * image_pre * image))
     kzs[...] = mine
@@ -388,7 +383,7 @@
         in_specs=[anywhere] * 6,
         out_specs=vmem,
         scratch_shapes=[
-            pltpu.VMEM(design_matrix.shape, BF16),
+            pltpu.VMEM(design_matrix.shape, BF16), pltpu.VMEM(design_matrix.shape, BF16),
             pltpu.VMEM((1, design_matrix.shape[0]), jnp.int32), pltpu.VMEM((k, half), F32), pltpu.VMEM((1, k), F32),
             pltpu.VMEM((rank,), F32),
             pltpu.VMEM((nx * nh, half, rank), BF16),
@@ -406,12 +401,10 @@
             pltpu.VMEM((2, ny, 1, rank), F32), pltpu.VMEM((2, ny, 1, rank), F32),
             pltpu.VMEM((2, nzx, 1, rank + wide), F32), pltpu.VMEM((2, 1, rank + wide), F32),
             pltpu.VMEM((2, ny, 1, rank + wide), F32), pltpu.VMEM((2, 1, rank + wide), F32),
-            pltpu.VMEM((nz, k, nx * wide), BF16), pltpu.VMEM((k, nx * wide), BF16),
-            pltpu.VMEM((nx, k, wide), F32),
-            pltpu.VMEM((nx, k, nz * wide), BF16), pltpu.VMEM((k, nz * wide), BF16),
+            pltpu.VMEM((2, nx, k, nz * wide), BF16), pltpu.VMEM((2, k, nz * wide), BF16),
             pltpu.VMEM((nz, k, wide), F32),
             pltpu.VMEM((nzx * nh, 1, wide), F32), pltpu.VMEM((1, wide), F32),
-            dma((6,)), dma((27,)), dma((27,)), dma((4, nz)), dma((nz // 2, 2)),
+            dma((7,)), dma((28,)), dma((28,)), dma((3, nz)), dma((nz // 2, 2)), dma((2, nx)),
         ],
         compiler_params=pltpu.CompilerParams(collective_id=0, has_side_effects=True),
     )(design_matrix, labels.reshape(1, -1), weights, lambdas.reshape(1, -1), sketch, sketch_values)

time: 104 us -> 101 us (0.971)
  Pallas kernels: 103 us -> 99.6 us
    pallas_call x1, Pallas kernels: 103 us -> 99.6 us  [shards(): pl.pallas_call(functools.partial(kernel, sizes), name='step', out_shape=j...]
where the time goes in v7:
time: 101 us
  Pallas kernels  99.6 us (99%)
  local copies, waits for them, and re-layouts  1.3 us (1%)
    pallas_call x1, Pallas kernels, shards(): pl.pallas_call(functools.partial(kernel, sizes), name='step', out_shape=j...  99.6 us

profile of v7, /device:TPU:1, one launch (start us, length us, event | category | flops | bytes accessed | tf_op | source)
XLA Modules:
  0.0 100.9 jit_solution(10971222471140244726)
XLA Ops:
  0.0 99.6 %step.1 = f32[16,64]{1,0:T(8,128)} custom-call(bf16[128,4096]{1,0:T(8,128)(2,1)} %x_hbm.1, s32[1,128]{1,0:T(1,128)} %bitcast.2, f32[16,64]{1,0:T(8,128)} %w_hbm.1, f32[1,16]{1,0:T(1,128)} %bitcast.3, bf16[64,384]{1,0:T(8,128)(2,1)} %s_hbm.1, f32[384]{0:T(512)} %sv_hbm.1), custom_call_target="tpu_custom_call" | custom-call | tf_op jit(solution)/shard_map/step/pallas_call | solution.py:379
  99.6 1.3 %copy.8 = f32[16,64]{1,0:T(8,128)} copy(f32[16,64]{1,0:T(8,128)} %step.1) | data formatting | bytes 8192

commit v8 on v7

--- a/solution.py
+++ b/solution.py
@@ -56,14 +56,16 @@
                         f_peers.append((ll * nc + cc, {"feat_0": ll, "feat_1": cc}))
     partner = {"samp_2": 1 - h}
 
+    loads = [pltpu.make_async_copy(src, dst, local_sem.at[j]) for j, (src, dst) in enumerate(
+        [(w_hbm, w_ref), (lam_hbm, lam_ref), (sv_hbm, sv_ref), (labels_hbm, labels_ref), (s_hbm, sp.at[x * nh + h]), (x_hbm, xv)])]
+    loads[0].start()
+    loads[4].start()
     barrier = pltpu.get_barrier_semaphore()
     for _, peer in zx_peers + y_peers:
         pl.semaphore_signal(barrier, inc=1, device_id=peer, device_id_type=pl.DeviceIdType.MESH)
 
-    loads = [pltpu.make_async_copy(src, dst, local_sem.at[j]) for j, (src, dst) in enumerate(
-        [(w_hbm, w_ref), (lam_hbm, lam_ref), (sv_hbm, sv_ref), (labels_hbm, labels_ref), (s_hbm, sp.at[x * nh + h]), (x_hbm, xv)])]
-    for load in loads:
-        load.start()
+    for j in (1, 2, 3, 5):
+        loads[j].start()
     for q in range(nx):
         for zz in range(nz):
             pltpu.make_async_copy(x_hbm.at[:, pl.ds((zz * nx + q) * wide, wide)], xw.at[:, pl.ds((q * nz + zz) * wide, wide)],
@@ -179,6 +181,10 @@
             copy(5 + i, fts.at[i], ft.at[i, f], peer).start()
         if i == 0:
             whole(27, sp.at[x * nh + 1 - h], partner)
+            block = sp.at[pl.ds(x * nh, nh)]
+            for dx in far_first(nx):
+                if dx:
+                    copy(1, block, block, {"samp_1": lax.rem(x + dx, nx)}).start()
             ring(1)
         whole(5 + i, ft.at[i, pl.ds(0, nf - 1)], f_peers[0][1])
         return jnp.sum(ft[i], axis=0)
@@ -304,27 +310,23 @@
         whole(18 + i, pa.at[i, pl.ds(0, ny - 1), :, across], y_peers[0][1])
         return vector, image, jnp.concatenate([pa[i, q, :, across] for q in range(k)], axis=0)
 
-    for load in loads[:4]:
-        load.wait()
-    lam = jnp.sum(jnp.where(lax.broadcasted_iota(jnp.int32, (k, k), 0) == lax.broadcasted_iota(jnp.int32, (k, k), 1),
-                            lam_ref[...], 0.0), axis=1, keepdims=True)
-    values = sv_ref[...].reshape(1, rank)
-    ratios = (jnp.min(values, axis=1, keepdims=True) + lam) / (values + lam) - 1.0
+    loads[0].wait()
     wb[0, :, :half] = w_ref[...]
     wb[0, :, half:] = w_ref[...]
     pl.semaphore_wait(barrier, len(zx_peers) + len(y_peers))
     copy(0, wb.at[0], wb.at[1], partner).start()
     loads[4].wait()
     copy(27, sp.at[x * nh + h], sp.at[x * nh + h], partner).start()
+    for load in loads[1:4]:
+        load.wait()
+    lam = jnp.sum(jnp.where(lax.broadcasted_iota(jnp.int32, (k, k), 0) == lax.broadcasted_iota(jnp.int32, (k, k), 1),
+                            lam_ref[...], 0.0), axis=1, keepdims=True)
+    values = sv_ref[...].reshape(1, rank)
+    ratios = (jnp.min(values, axis=1, keepdims=True) + lam) / (values + lam) - 1.0
     whole(0, wb.at[1], partner)
     own = (lane // half) == h
     weights = jnp.where(own, wb[0], wb[1])
     gather_start(0, weights)
-    for dh in reversed(range(nh)):
-        for dx in far_first(nx):
-            if dx:
-                peer = {"samp_1": lax.rem(x + dx, nx), "samp_2": lax.rem(h + dh, nh)}
-                copy(1, sp.at[x * nh + h], sp.at[x * nh + h], peer).start()
     loads[5].wait()
     pltpu.make_async_copy(x_hbm, xw, local_sem.at[6]).wait()
 

time: 101 us -> 101 us (level)
  no operation moved by 1% of the time
where the time goes in v8:
time: 101 us
  Pallas kernels  99.7 us (99%)
  local copies, waits for them, and re-layouts  1.3 us (1%)
    pallas_call x1, Pallas kernels, shards(): pl.pallas_call(functools.partial(kernel, sizes), name='step', out_shape=j...  99.7 us

profile of v8, /device:TPU:1, one launch (start us, length us, event | category | flops | bytes accessed | tf_op | source)
XLA Modules:
  0.0 101.0 jit_solution(11816585311069026116)
XLA Ops:
  0.0 99.7 %step.1 = f32[16,64]{1,0:T(8,128)} custom-call(bf16[128,4096]{1,0:T(8,128)(2,1)} %x_hbm.1, s32[1,128]{1,0:T(1,128)} %bitcast.2, f32[16,64]{1,0:T(8,128)} %w_hbm.1, f32[1,16]{1,0:T(1,128)} %bitcast.3, bf16[64,384]{1,0:T(8,128)(2,1)} %s_hbm.1, f32[384]{0:T(512)} %sv_hbm.1), custom_call_target="tpu_custom_call" | custom-call | tf_op jit(solution)/shard_map/step/pallas_call | solution.py:381
  99.7 1.3 %copy.8 = f32[16,64]{1,0:T(8,128)} copy(f32[16,64]{1,0:T(8,128)} %step.1) | data formatting | bytes 8192

commit v9 on v8

--- a/solution.py
+++ b/solution.py
@@ -408,8 +408,9 @@
             pltpu.VMEM((nzx * nh, 1, wide), F32), pltpu.VMEM((1, wide), F32),
             dma((7,)), dma((28,)), dma((28,)), dma((3, nz)), dma((nz // 2, 2)), dma((2, nx)),
         ],
-        compiler_params=pltpu.CompilerParams(collective_id=0, has_side_effects=True),
-    )(design_matrix, labels.reshape(1, -1), weights, lambdas.reshape(1, -1), sketch, sketch_values)
+        compiler_params=pltpu.CompilerParams(collective_id=0, has_side_effects=True, vmem_limit_bytes=32 << 20),
+    )(*(pltpu.with_memory_space_constraint(operand, pltpu.HBM) for operand in (
+        design_matrix, labels.reshape(1, -1), weights, lambdas.reshape(1, -1), sketch, sketch_values)))
 
 
 def solution(mesh):

time: 101 us -> 99.8 us (0.988)
  no operation moved by 1% of the time
where the time goes in v9:
time: 99.8 us; the launch traced here: 99.7 us
  Pallas kernels  99.1 us (99%)
    pallas_call x1, Pallas kernels, shards(): pl.pallas_call(functools.partial(kernel, sizes), name='step', out_shape=j...  99.1 us

profile of v9, /device:TPU:1, one launch (start us, length us, event | category | flops | bytes accessed | tf_op | source)
XLA Modules:
  0.0 99.7 jit_solution(1681332028461644533)
XLA Ops:
  0.0 99.1 %step.1 = f32[16,64]{1,0:T(8,128)S(1)} custom-call(bf16[128,4096]{1,0:T(8,128)(2,1)} %x_hbm.1, s32[1,128]{1,0:T(1,128)} %bitcast.2, f32[16,64]{1,0:T(8,128)} %w_hbm.1, f32[1,16]{1,0:T(1,128)} %bitcast.3, bf16[64,384]{1,0:T(8,128)(2,1)} %s_hbm.1, f32[384]{0:T(512)} %sv_hbm.1), custom_call_target="tpu_custom_call" | custom-call | tf_op jit(solution)/shard_map/step/pallas_call | solution.py:381
  99.1 0.6 copy.8

commit v10 on v9

--- a/solution.py
+++ b/solution.py
@@ -233,10 +233,10 @@
                 copy(21, xs.at[xx], xr.at[x], {"samp_1": xx}).start()
         xr[x] = xs[x]
         whole(21, xr.at[pl.ds(0, nx - 1)], {"samp_1": lax.rem(x + 1, nx)})
-        vector, image, full = project_finish(0, jnp.sum(xr[...], axis=0), None)
+        vector, full = project_finish(0, jnp.sum(xr[...], axis=0), None)
         ring(5)
         spread_start(0, spread(full))
-        return vector, vector + cf[z], image
+        return vector, vector + cf[z], gather_rows(1)
 
     def along_x(values, state, scalars):
         for dx in far_first(nx):
@@ -260,9 +260,9 @@
                 copy(22, zs.at[zz], zr.at[z], {"samp_0": zz}).start()
         zr[z] = zs[z]
         whole(22, zr.at[pl.ds(0, nz - 1)], zx_peers[0][1])
-        vector, image, full = project_finish(1, jnp.sum(zr[...], axis=0), scalars)
+        vector, full = project_finish(1, jnp.sum(zr[...], axis=0), scalars)
         spread_start(1, spread(full))
-        return vector, vector + cf[z], image, jnp.sum(full[:, rank:], axis=0, keepdims=True) * (1.0 / nf)
+        return vector, vector + cf[z], gather_rows(2), jnp.sum(full[:, rank:], axis=0, keepdims=True) * (1.0 / nf)
 
     def project_start(i, chunks, sketch):
         parts = lax.dot_general(split3(jnp.concatenate(chunks, axis=1)), sketch, BY_ROWS, preferred_element_type=F32)
@@ -296,7 +296,6 @@
 
         whole(12 + i, yh.at[i], partner)
         vector = part + yh[i]
-        gather_start(1 + i, vector)
 
         whole(16 + i, pz.at[i, pl.ds(0, nzx - 1), :, across], zx_peers[0][1])
         mine = jnp.sum(pz[i, :, :, across], axis=0)
@@ -304,11 +303,11 @@
         pa[i, y, :, across] = mine
         for _, peer in y_peers:
             copy(18 + i, pas.at[i, :, across], pa.at[i, y, :, across], peer).start()
+        gather_start(1 + i, vector)
         if i == 0:
             ring(4)
-        image = gather_rows(1 + i)
         whole(18 + i, pa.at[i, pl.ds(0, ny - 1), :, across], y_peers[0][1])
-        return vector, image, jnp.concatenate([pa[i, q, :, across] for q in range(k)], axis=0)
+        return vector, jnp.concatenate([pa[i, q, :, across] for q in range(k)], axis=0)
 
     loads[0].wait()
     wb[0, :, :half] = w_ref[...]

time: 99.8 us -> 101 us (1.012)
  no operation moved by 1% of the time
where the time goes in v10:
time: 101 us; the launch traced here: 100 us
  Pallas kernels  99.8 us (99%)
    pallas_call x1, Pallas kernels, shards(): pl.pallas_call(functools.partial(kernel, sizes), name='step', out_shape=j...  99.8 us

profile of v10, /device:TPU:1, one launch (start us, length us, event | category | flops | bytes accessed | tf_op | source)
XLA Modules:
  0.0 100.4 jit_solution(5250026728797296577)
XLA Ops:
  0.0 99.8 %step.1 = f32[16,64]{1,0:T(8,128)S(1)} custom-call(bf16[128,4096]{1,0:T(8,128)(2,1)} %x_hbm.1, s32[1,128]{1,0:T(1,128)} %bitcast.2, f32[16,64]{1,0:T(8,128)} %w_hbm.1, f32[1,16]{1,0:T(1,128)} %bitcast.3, bf16[64,384]{1,0:T(8,128)(2,1)} %s_hbm.1, f32[384]{0:T(512)} %sv_hbm.1), custom_call_target="tpu_custom_call" | custom-call | tf_op jit(solution)/shard_map/step/pallas_call | solution.py:380
  99.8 0.6 copy.8

commit v11 on v10

--- a/solution.py
+++ b/solution.py
@@ -121,6 +121,9 @@
     def gather_rows(i):
         total = jnp.zeros((k, xv.shape[0]), F32)
         for dz in reversed(far_first(nz)):
+            if i == 0 and dz == nz // 2:
+                whole(27, sp.at[x * nh + 1 - h], partner)
+                ring(1)
             arrived_group(2 + i, i, dz, ag.at[i, pl.ds(0, nx if dz else nx - 1)])
             zz = lax.rem(z + (nz - dz), nz)
             total = total + rows_of(jnp.concatenate([ag[i, zz * nx + q] for q in range(nx)], axis=1), zz)
@@ -180,12 +183,11 @@
         for _, peer in f_peers:
             copy(5 + i, fts.at[i], ft.at[i, f], peer).start()
         if i == 0:
-            whole(27, sp.at[x * nh + 1 - h], partner)
             block = sp.at[pl.ds(x * nh, nh)]
             for dx in far_first(nx):
                 if dx:
                     copy(1, block, block, {"samp_1": lax.rem(x + dx, nx)}).start()
-            ring(1)
+            ring(2)
         whole(5 + i, ft.at[i, pl.ds(0, nf - 1)], f_peers[0][1])
         return jnp.sum(ft[i], axis=0)
 
@@ -221,7 +223,7 @@
         chunks = [total[:, q * wide:(q + 1) * wide] + ridge * jnp.where(x == q, 1.0, 0.0) for q in range(nx)]
         whole(1, sp.at[pl.ds(0, (nx - 1) * nh)], partner)
         project_start(0, chunks, sp[...].reshape(nx * nh * half, rank))
-        ring(2)
+        ring(3)
 
         whole(25, rl.at[pl.ds(0, nz - 1)], zx_peers[0][1])
         low = jnp.sum(rl[...].astype(F32), axis=0)
@@ -291,8 +293,6 @@
         pz[i, zx, :, across] = mine
         for _, peer in zx_peers:
             copy(16 + i, pzs.at[i, :, across], pz.at[i, zx, :, across], peer).start()
-        if i == 0:
-            ring(3)
 
         whole(12 + i, yh.at[i], partner)
         vector = part + yh[i]

time: 101 us -> 103 us (1.020)
  Pallas kernels: 99.8 us -> 102 us
    pallas_call x1, Pallas kernels: 99.8 us -> 102 us  [shards(): pl.pallas_call(functools.partial(kernel, sizes), name='step', out_shape=j...]
where the time goes in v11:
time: 103 us
  Pallas kernels  102 us (99%)
    pallas_call x1, Pallas kernels, shards(): pl.pallas_call(functools.partial(kernel, sizes), name='step', out_shape=j...  102 us

profile of v11, /device:TPU:1, one launch (start us, length us, event | category | flops | bytes accessed | tf_op | source)
XLA Modules:
  0.0 102.9 jit_solution(7086803549967748357)
XLA Ops:
  0.0 102.3 %step.1 = f32[16,64]{1,0:T(8,128)S(1)} custom-call(bf16[128,4096]{1,0:T(8,128)(2,1)} %x_hbm.1, s32[1,128]{1,0:T(1,128)} %bitcast.2, f32[16,64]{1,0:T(8,128)} %w_hbm.1, f32[1,16]{1,0:T(1,128)} %bitcast.3, bf16[64,384]{1,0:T(8,128)(2,1)} %s_hbm.1, f32[384]{0:T(512)} %sv_hbm.1), custom_call_target="tpu_custom_call" | custom-call | tf_op jit(solution)/shard_map/step/pallas_call | solution.py:380
  102.3 0.6 copy.8

commit v12 on v10

--- a/solution.py
+++ b/solution.py
@@ -29,7 +29,7 @@
 
 
 def kernel(sizes, x_hbm, labels_hbm, w_hbm, lam_hbm, s_hbm, sv_hbm, out_ref,
-           xv, xw, labels_ref, w_ref, lam_ref, sv_ref, sp, wb, ag, ags, ft, fts, fs, fss, rs, rss, rl, rls, ws, wss, xr, xs, zr, zs, spz, yh, yhs,
+           xv, xw, labels_ref, w_ref, lam_ref, sv_ref, sp, wb, ag, ags, ft, fts, fs, fss, rs, rss, rl, rls, lz, lzs, ws, wss, xr, xs, zr, zs, spz, yh, yhs,
            pr, prs, pz, pzs, pa, pas, cx, cxs, cf, kz, kzs, local_sem, send_sem, recv_sem, gather_sem, ring_sem, x_sem):
     nz, nx, nh, nl, nc = sizes
     nzx, nf, ny = nz * nx, nl * nc, nh * nl * nc
@@ -206,15 +206,17 @@
             part = lax.dot_general(values, xv[:, pl.ds(start, nx * wide)], BY_ROWS, preferred_element_type=F32)
             high = part.astype(BF16)
             rss[zz] = high
-            rls[zz] = (part - high.astype(F32)).astype(BF16)
+            low = (part - high.astype(F32)).astype(BF16)
+            for q in range(nx):
+                rls[q, :, pl.ds(pl.multiple_of(zz * wide, wide), wide)] = low[:, q * wide:(q + 1) * wide]
             if dz:
                 copy(10, rss.at[zz], rs.at[z], {"samp_0": zz}).start()
         rs[z] = rss[z]
-        for dz in far_first(nz):
-            zz = lax.rem(z + dz, nz)
-            if dz:
-                copy(25, rls.at[zz], rl.at[z], {"samp_0": zz}).start()
-        rl[z] = rls[z]
+        for dx in far_first(nx):
+            xx = lax.rem(x + dx, nx)
+            if dx:
+                copy(25, rls.at[xx], rl.at[x], {"samp_1": xx}).start()
+        rl[x] = rls[x]
         whole(10, rs.at[pl.ds(0, nz - 1)], zx_peers[0][1])
         total = jnp.sum(rs[...].astype(F32), axis=0)
         ridge = (0.5 * lam) * state
@@ -223,17 +225,25 @@
         project_start(0, chunks, sp[...].reshape(nx * nh * half, rank))
         ring(2)
 
-        whole(25, rl.at[pl.ds(0, nz - 1)], zx_peers[0][1])
+        whole(25, rl.at[pl.ds(0, nx - 1)], {"samp_1": lax.rem(x + 1, nx)})
         low = jnp.sum(rl[...].astype(F32), axis=0)
+        for q in range(nz):
+            lzs[q] = low[:, q * wide:(q + 1) * wide]
+        for dz in far_first(nz):
+            zz = lax.rem(z + dz, nz)
+            if dz:
+                copy(28, lzs.at[zz], lz.at[z], {"samp_0": zz}).start()
+        lz[z] = lzs[z]
         for q in range(nx):
-            xs[q] = chunks[q] + low[:, q * wide:(q + 1) * wide]
+            xs[q] = chunks[q]
         for dx in far_first(nx):
             xx = lax.rem(x + dx, nx)
             if dx:
                 copy(21, xs.at[xx], xr.at[x], {"samp_1": xx}).start()
         xr[x] = xs[x]
         whole(21, xr.at[pl.ds(0, nx - 1)], {"samp_1": lax.rem(x + 1, nx)})
-        vector, full = project_finish(0, jnp.sum(xr[...], axis=0), None)
+        whole(28, lz.at[pl.ds(0, nz - 1)], zx_peers[0][1])
+        vector, full = project_finish(0, jnp.sum(xr[...], axis=0) + jnp.sum(lz[...], axis=0), None)
         ring(5)
         spread_start(0, spread(full))
         return vector, vector + cf[z], gather_rows(1)
@@ -393,7 +403,8 @@
             pltpu.VMEM((3, nf, k, wide), F32), pltpu.VMEM((3, k, wide), F32),
             pltpu.VMEM((2, nf, 1, wide), F32), pltpu.VMEM((2, 1, wide), F32),
             pltpu.VMEM((nz, k, nx * wide), BF16), pltpu.VMEM((nz, k, nx * wide), BF16),
-            pltpu.VMEM((nz, k, nx * wide), BF16), pltpu.VMEM((nz, k, nx * wide), BF16),
+            pltpu.VMEM((nx, k, nz * wide), BF16), pltpu.VMEM((nx, k, nz * wide), BF16),
+            pltpu.VMEM((nz, k, wide), F32), pltpu.VMEM((nz, k, wide), F32),
             pltpu.VMEM((nx, k, nz * wide), BF16), pltpu.VMEM((nx, k, nz * wide), BF16),
             pltpu.VMEM((nx, k, wide), F32), pltpu.VMEM((nx, k, wide), F32),
             pltpu.VMEM((nz, k, wide), F32), pltpu.VMEM((nz, k, wide), F32),
@@ -405,7 +416,7 @@
             pltpu.VMEM((2, nx, k, nz * wide), BF16), pltpu.VMEM((2, k, nz * wide), BF16),
             pltpu.VMEM((nz, k, wide), F32),
             pltpu.VMEM((nzx * nh, 1, wide), F32), pltpu.VMEM((1, wide), F32),
-            dma((7,)), dma((28,)), dma((28,)), dma((3, nz)), dma((nz // 2, 2)), dma((2, nx)),
+            dma((7,)), dma((29,)), dma((29,)), dma((3, nz)), dma((nz // 2, 2)), dma((2, nx)),
         ],
         compiler_params=pltpu.CompilerParams(collective_id=0, has_side_effects=True, vmem_limit_bytes=32 << 20),
     )(*(pltpu.with_memory_space_constraint(operand, pltpu.HBM) for operand in (

time: 101 us -> 100 us (0.990)
  no operation moved by 1% of the time
where the time goes in v12:
time: 100 us
  Pallas kernels  99.6 us (100%)
    pallas_call x1, Pallas kernels, shards(): pl.pallas_call(functools.partial(kernel, sizes), name='step', out_shape=j...  99.6 us

profile of v12, /device:TPU:1, one launch (start us, length us, event | category | flops | bytes accessed | tf_op | source)
XLA Modules:
  0.0 100.2 jit_solution(9458274524976718040)
XLA Ops:
  0.0 99.6 %step.1 = f32[16,64]{1,0:T(8,128)S(1)} custom-call(bf16[128,4096]{1,0:T(8,128)(2,1)} %x_hbm.1, s32[1,128]{1,0:T(1,128)} %bitcast.2, f32[16,64]{1,0:T(8,128)} %w_hbm.1, f32[1,16]{1,0:T(1,128)} %bitcast.3, bf16[64,384]{1,0:T(8,128)(2,1)} %s_hbm.1, f32[384]{0:T(512)} %sv_hbm.1), custom_call_target="tpu_custom_call" | custom-call | tf_op jit(solution)/shard_map/step/pallas_call | solution.py:390
  99.6 0.6 copy.8

commit v13 on v9

--- a/solution.py
+++ b/solution.py
@@ -61,7 +61,7 @@
     loads[0].start()
     loads[4].start()
     barrier = pltpu.get_barrier_semaphore()
-    for _, peer in zx_peers + y_peers:
+    for _, peer in [y_peers[-2]] + zx_peers + y_peers[:-2] + y_peers[-1:]:
         pl.semaphore_signal(barrier, inc=1, device_id=peer, device_id_type=pl.DeviceIdType.MESH)
 
     for j in (1, 2, 3, 5):

time: 99.8 us -> 100 us (level)
  no operation moved by 1% of the time
where the time goes in v13:
time: 100 us; the launch traced here: 99.9 us
  Pallas kernels  99.2 us (99%)
    pallas_call x1, Pallas kernels, shards(): pl.pallas_call(functools.partial(kernel, sizes), name='step', out_shape=j...  99.2 us

profile of v13, /device:TPU:1, one launch (start us, length us, event | category | flops | bytes accessed | tf_op | source)
XLA Modules:
  0.0 99.9 jit_solution(8826148733963109548)
XLA Ops:
  0.0 99.2 %step.1 = f32[16,64]{1,0:T(8,128)S(1)} custom-call(bf16[128,4096]{1,0:T(8,128)(2,1)} %x_hbm.1, s32[1,128]{1,0:T(1,128)} %bitcast.2, f32[16,64]{1,0:T(8,128)} %w_hbm.1, f32[1,16]{1,0:T(1,128)} %bitcast.3, bf16[64,384]{1,0:T(8,128)(2,1)} %s_hbm.1, f32[384]{0:T(512)} %sv_hbm.1), custom_call_target="tpu_custom_call" | custom-call | tf_op jit(solution)/shard_map/step/pallas_call | solution.py:381
  99.3 0.6 copy.8
